TPU v7x, 256 devices: a whole 4x4x8 slice. The times are simulated.
256 devices in a mesh: dp: 16 (over x, y_lo, core), seq: 16 (over y_hi, z).
Axes of the slice: x: 4, y: 4 (y_hi: 2, y_lo: 2; y = y_hi * 2 + y_lo), z: 8, core: 2. Of those that a mesh axis runs over, the one named last changes fastest.
Arguments:
- query: bfloat16 [16, 2048, 2048], P('dp', 'seq'), may hold values from -8 to 8
- key_value: bfloat16 [2, 16, 2048, 2048], P(None, 'dp', 'seq'), may hold values from -8 to 8
- grad_y: bfloat16 [16, 2048, 2048], P('dp', 'seq'), may hold values from -6 to 6
- tags: int32 [16, 2048], P('dp', 'seq'), may hold values 0 or 1
- segments: int32 [16, 2048], P('dp'), may hold values from 0 to 15, never falling along the last dimension, each value on 1 to 256 neighbouring positions
- out_weight: bfloat16 [2, 2048, 2048], P(None, None, 'dp'), may hold values from -0.125 to 0.125
Outputs:
- grad_query: bfloat16 [16, 2048, 2048], P('dp', 'seq')
- grad_key_value: bfloat16 [2, 16, 2048, 2048], P(None, 'dp', 'seq')
Inputs may be any that keep to these rules, and one draw needn't show every extreme that they name: `segments`: sample numbers never fall along a sequence; a sample holds at most 256 positions and some sample holds exactly 256.
All inputs are finite; a program needn't handle non-finite values. No bound on the sum of `tags` on one device may be relied on, other than what follows from the above.
Results may differ from a plain program's by a relative error of at most 0.0075.
Values may be sent and summed in bfloat16 or wider, within the bound.
A program may use at most 128 MiB of HBM per device.

v0:
```python
import jax
import jax.numpy as jnp
from jax import lax
from jax.sharding import PartitionSpec as P

HEADS = 16
HEAD_DIM = 128
REACH = 2


NEG = -1e30


def passed_along(value, axis, steps):
    count = lax.axis_size(axis)
    first, last = (max(0, -steps), min(count, count - steps))
    return lax.ppermute(value, axis, [(source, source + steps) for source in range(first, last)])


def local_grads(query, keys, values, grad_out, mask, scale):
    scores = jnp.einsum("qhe,khe->hqk", query, keys, preferred_element_type=jnp.float32) * scale
    scores = jnp.where(mask[None], scores, NEG)
    top = jnp.max(scores, axis=2, keepdims=True)
    lse = top + jnp.log(jnp.sum(jnp.exp(scores - top), axis=2, keepdims=True))
    probs = jnp.exp(scores - lse)
    probs_low = probs.astype(jnp.bfloat16)
    dprob = jnp.einsum("qhe,khe->hqk", grad_out, values, preferred_element_type=jnp.float32)
    delta = jnp.sum(probs * dprob, axis=2, keepdims=True)
    dscore = (probs * (dprob - delta) * scale).astype(jnp.bfloat16)
    grad_q = jnp.einsum("hqk,khe->qhe", dscore, keys, preferred_element_type=jnp.float32)
    grad_k = jnp.einsum("hqk,qhe->khe", dscore, query, preferred_element_type=jnp.float32)
    grad_v = jnp.einsum("hqk,qhe->khe", probs_low, grad_out, preferred_element_type=jnp.float32)
    return (grad_q, grad_k, grad_v, lse[:, :, 0], delta[:, :, 0])


def flatten(array):
    return array.reshape((array.shape[0], array.shape[1] * array.shape[2]))


def shards(query, key_value, grad_y, tags, segments, out_weight):
    rows = query.shape[1]
    group = min(4, HEADS)
    span = group * HEAD_DIM
    blocks = HEADS // group
    scale = HEAD_DIM ** (-0.5)
    index = lax.axis_index("seq")
    count = lax.axis_size("seq")
    own_q = query[0]
    own_kv = key_value[:, 0]
    grad = grad_y[0]
    is_text = tags[0] == 1
    seg_all = segments[0]

    def seg_block(number):
        return lax.dynamic_slice_in_dim(seg_all, jnp.clip(number, 0, count - 1) * rows, rows)

    seg_own = seg_block(index)
    causal = jnp.arange(rows)[:, None] >= jnp.arange(rows)[None, :]
    mask_parts = []
    for back in range(REACH, 0, -1):
        mask_parts.append(
            (seg_own[:, None] == seg_block(index - back)[None, :]) & (index - back >= 0)
        )
    mask_parts.append((seg_own[:, None] == seg_own[None, :]) & causal)
    mask_window = jnp.concatenate(mask_parts, axis=1)
    piece = lax.all_gather(out_weight, "dp", axis=2, tiled=True)
    text_part = jnp.einsum("td,hd->th", grad, piece[1], preferred_element_type=jnp.float32)
    image_part = jnp.einsum("td,hd->th", grad, piece[0], preferred_element_type=jnp.float32)
    grad_out = jnp.where(is_text[:, None], text_part, image_part).astype(jnp.bfloat16)
    befores = []
    current = own_kv
    for back in range(REACH):
        current = passed_along(current, "seq", 1)
        befores.append(current)

    def heads_of(array, number):
        return array[..., number * span : (number + 1) * span].reshape(
            array.shape[:-1] + (group, HEAD_DIM)
        )

    query_parts, lse_parts, delta_parts = ([], [], [])
    key_terms = [[] for back in range(REACH + 1)]
    value_terms = [[] for back in range(REACH + 1)]
    for number in range(blocks):
        window = [heads_of(befores[back], number) for back in range(REACH - 1, -1, -1)]
        window.append(heads_of(own_kv, number))
        keys = jnp.concatenate([item[0] for item in window], axis=0)
        values = jnp.concatenate([item[1] for item in window], axis=0)
        grad_q, grad_k, grad_v, lse, delta = local_grads(
            heads_of(own_q, number), keys, values, heads_of(grad_out, number), mask_window, scale
        )
        query_parts.append(flatten(grad_q))
        for back in range(REACH + 1):
            place = REACH - back
            key_terms[back].append(flatten(grad_k[place * rows : (place + 1) * rows]))
            value_terms[back].append(flatten(grad_v[place * rows : (place + 1) * rows]))
        lse_parts.append(lse)
        delta_parts.append(delta)
    terms = [
        jnp.stack(
            [jnp.concatenate(key_terms[back], axis=1), jnp.concatenate(value_terms[back], axis=1)]
        )
        for back in range(REACH + 1)
    ]
    carried = terms[REACH]
    for back in range(REACH - 1, -1, -1):
        carried = (
            passed_along(carried.astype(jnp.bfloat16), "seq", -1).astype(carried.dtype)
            + terms[back]
        )
    grad_query = jnp.concatenate(query_parts, axis=1).astype(jnp.bfloat16)[None]
    return (grad_query, carried.astype(jnp.bfloat16)[:, None])


def solution(mesh):
    return jax.shard_map(
        shards,
        mesh=mesh,
        in_specs=(
            P("dp", "seq", None),
            P(None, "dp", "seq", None),
            P("dp", "seq", None),
            P("dp", "seq"),
            P("dp", None),
            P(None, None, "dp"),
        ),
        out_specs=(P("dp", "seq", None), P(None, "dp", "seq", None)),
        check_vma=False,
    )
```

profile of v0, /device:TPU:1, one launch (start us, length us, event | category | flops | bytes accessed | tf_op | source)
XLA Modules:
  0.0 283.3 jit_solution(14988529724436020839)
XLA Ops:
  9.5 4.4 %collective-permute-start = (bf16[2,128,2048]{1,2,0:T(8,128)(2,1)S(1)}, bf16[2,128,2048]{1,2,0:T(8,128)(2,1)S(1)}, u32[]{:S(2)}, u32[]{:S(2)}) collective-permute-start(bf16[2,128,2048]{1,2,0:T(8,128)(2,1)S(1)} %bitcast.155), channel_id=1, source_target_pairs={{0,1},{1,2},{2,3},{3,4},{4,5},{5,6},{6,7},{7,8},{8,9},{9,10},{10,1... | collective-permute-start | bytes 3145736 | tf_op jit(solution)/shard_map/ppermute | solution.py:17
  25.6 10.1 %collective-permute-done = bf16[2,128,2048]{1,2,0:T(8,128)(2,1)S(1)} collective-permute-done((bf16[2,128,2048]{1,2,0:T(8,128)(2,1)S(1)}, bf16[2,128,2048]{1,2,0:T(8,128)(2,1)S(1)}, u32[]{:S(2)}, u32[]{:S(2)}) %collective-permute-start) | collective-permute-done | bytes 1048608 | tf_op jit(solution)/shard_map/ppermute | solution.py:17
  35.7 4.3 %collective-permute-start.1 = (bf16[2,128,2048]{1,2,0:T(8,128)(2,1)S(1)}, bf16[2,128,2048]{1,2,0:T(8,128)(2,1)S(1)}, u32[]{:S(2)}, u32[]{:S(2)}) collective-permute-start(bf16[2,128,2048]{1,2,0:T(8,128)(2,1)S(1)} %collective-permute-done), channel_id=1, source_target_pairs={{0,1},{1,2},{2,3},{3,4},{4,5},{5,6},{6,7},{7,8},{8,9},{9,10},{10,1... | collective-permute-start | bytes 3145736 | tf_op jit(solution)/shard_map/ppermute | solution.py:17
  52.5 8.5 %collective-permute-done.1 = bf16[2,128,2048]{1,2,0:T(8,128)(2,1)S(1)} collective-permute-done((bf16[2,128,2048]{1,2,0:T(8,128)(2,1)S(1)}, bf16[2,128,2048]{1,2,0:T(8,128)(2,1)S(1)}, u32[]{:S(2)}, u32[]{:S(2)}) %collective-permute-start.1) | collective-permute-done | bytes 1048608 | tf_op jit(solution)/shard_map/ppermute | solution.py:17
  69.1 84.0 %all-gather.2.cloned.1.call-done = bf16[2,2048,2048]{2,1,0:T(8,128)(2,1)} async-done(((bf16[2,2048,128]{2,1,0:T(8,128)(2,1)}), bf16[2,2048,2048]{2,1,0:T(8,128)(2,1)}) %all-gather.2.cloned.1.call-update) | async-done | bytes 16777232 | tf_op jit(solution)/shard_map/all_gather | solution.py:66
  153.1 6.3 %fusion.4 = bf16[128,2048]{1,0:T(8,128)(2,1)S(1)} fusion(bf16[2,2048,2048]{2,1,0:T(8,128)(2,1)} %all-gather.2.cloned.1.call-done, bf16[1,128,2048]{2,1,0:T(8,128)(2,1)S(1)} %copy-done), kind=kOutput, calls=%fused_computation.5 | convolution fusion | flops 1073741824 | bytes 9437184 | tf_op jit(solution)/shard_map/td,hd->th/dot_general | solution.py:68
  159.4 6.3 %fusion.7 = bf16[128,2048]{1,0:T(8,128)(2,1)S(1)} fusion(bf16[128,2048]{1,0:T(8,128)(2,1)S(1)} %fusion.4, bf16[2,2048,2048]{2,1,0:T(8,128)(2,1)} %all-gather.2.cloned.1.call-done, bf16[1,128,2048]{2,1,0:T(8,128)(2,1)S(1)} %copy-done, pred[128]{0:T(512)(128)(4,1)S(1)} %copy-done.49), kind=kOutput, calls=%fused_computation.9 | convolution fusion | flops 1074003968 | bytes 9961600 | tf_op jit(solution)/shard_map/td,hd->th/dot_general | solution.py:67
  166.6 2.4 convolution_bitcast_fusion
  170.1 3.3 %convolution_bitcast_fusion.4 = f32[384,4,128]{0,2,1:T(8,128)} fusion(bf16[128,4,128]{0,2,1:T(8,128)(2,1)S(1)} %bitcast.225, f32[4,128,384]{1,2,0:T(8,128)} %fusion.79, f32[4,128,384]{1,2,0:T(8,128)} %copy-done.2, f32[4,128]{1,0:T(4,128)S(1)} %log_add_fusion), kind=kOutput, calls=%fused_computation.30 | convolution fusion | flops 51708800 | bytes 2492416 | tf_op jit(solution)/shard_map/hqk,qhe->khe/dot_general | solution.py:31
  173.3 1.8 fusion.151
  179.3 2.8 convolution_bitcast_fusion.5
  182.0 1.8 fusion.150
  188.8 2.8 convolution_bitcast_fusion.6
  191.6 1.9 fusion.149
  197.8 2.8 convolution_bitcast_fusion.7
  200.6 1.9 fusion.148
  203.4 1.9 fusion.155
  209.3 1.7 copy.145
  223.5 1.8 copy.153
  225.3 1.8 copy.152
  227.1 1.9 fusion.153
  229.0 1.8 copy.151
  230.8 1.9 fusion.152
  232.7 1.8 copy.150
  234.5 3.2 %convolution_convert_fusion = bf16[4,128,128]{2,1,0:T(8,128)(2,1)} fusion(f32[4,128,384]{1,2,0:T(8,128)} %fusion.79, f32[4,128,384]{1,2,0:T(8,128)} %copy-done.2, f32[4,128]{1,0:T(4,128)S(1)} %log_add_fusion, bf16[128,4,128]{2,0,1:T(8,128)(2,1)S(1)} %copy-done.29, bf16[128,4,128]{2,0,1:T(8,128)(2,1)} %copy.111, bf16[128,4,128]{2,0,1:T(8,128)(2,1)} %copy-done.42), kind=kOutput, calls=%fused_computation.50 | convolution fusion | flops 52953984 | bytes 2099200 | tf_op jit(solution)/shard_map/hqk,khe->qhe/dot_general | solution.py:30
  239.0 6.3 %collective-permute-done.2 = bf16[2,128,2048]{2,1,0:T(8,128)(2,1)} collective-permute-done((bf16[2,128,2048]{2,1,0:T(8,128)(2,1)}, bf16[2,128,2048]{2,1,0:T(8,128)(2,1)}, u32[]{:S(2)}, u32[]{:S(2)}) %collective-permute-start.2) | collective-permute-done | bytes 1048608 | tf_op jit(solution)/shard_map/ppermute | solution.py:17
  245.3 2.6 fusion.8
  249.4 2.5 convolution_convert_fusion.1
  253.1 2.0 convolution_convert_fusion.2
  255.3 2.0 convolution_convert_fusion.3
  259.6 14.2 %collective-permute-done.3 = bf16[2,128,2048]{2,1,0:T(8,128)(2,1)} collective-permute-done((bf16[2,128,2048]{2,1,0:T(8,128)(2,1)}, bf16[2,128,2048]{2,1,0:T(8,128)(2,1)}, u32[]{:S(2)}, u32[]{:S(2)}) %collective-permute-start.3) | collective-permute-done | bytes 1048608 | tf_op jit(solution)/shard_map/ppermute | solution.py:17
  273.8 2.6 fusion.50
  (199 shorter events, 73.5 us)
Async XLA Ops:
  7.2 146.0 %copy-start = (bf16[1,128,2048]{2,1,0:T(8,128)(2,1)S(1)}, bf16[1,128,2048]{2,1,0:T(8,128)(2,1)}, u32[]{:S(2)}) copy-start(bf16[1,128,2048]{2,1,0:T(8,128)(2,1)} %param.8) | copy-start | bytes 1572868
  7.2 145.9 %all-gather.2.cloned.1.call-start = ((), (), s32[]{:S(2)}) async-start(), calls=%async_computation | async-start | bytes 17825792 | tf_op jit(solution)/shard_map/all_gather | solution.py:66
  9.5 26.2 %collective-permute-start = (bf16[2,128,2048]{1,2,0:T(8,128)(2,1)S(1)}, bf16[2,128,2048]{1,2,0:T(8,128)(2,1)S(1)}, u32[]{:S(2)}, u32[]{:S(2)}) collective-permute-start(bf16[2,128,2048]{1,2,0:T(8,128)(2,1)S(1)} %bitcast.155), channel_id=1, source_target_pairs={{0,1},{1,2},{2,3},{3,4},{4,5},{5,6},{6,7},{7,8},{8,9},{9,10},{10,1... | collective-permute-start | bytes 3145736 | tf_op jit(solution)/shard_map/ppermute | solution.py:17
  14.8 25.9 %copy-start.48 = (s32[1,128]{1,0:T(1,128)S(1)}, s32[1,128]{1,0:T(1,128)}, u32[]{:S(2)}) copy-start(s32[1,128]{1,0:T(1,128)} %param.9) | copy-start | bytes 1540
  35.7 25.3 %collective-permute-start.1 = (bf16[2,128,2048]{1,2,0:T(8,128)(2,1)S(1)}, bf16[2,128,2048]{1,2,0:T(8,128)(2,1)S(1)}, u32[]{:S(2)}, u32[]{:S(2)}) collective-permute-start(bf16[2,128,2048]{1,2,0:T(8,128)(2,1)S(1)} %collective-permute-done), channel_id=1, source_target_pairs={{0,1},{1,2},{2,3},{3,4},{4,5},{5,6},{6,7},{7,8},{8,9},{9,10},{10,1... | collective-permute-start | bytes 3145736 | tf_op jit(solution)/shard_map/ppermute | solution.py:17
  61.4 4.7 %copy-start.42 = (bf16[128,4,128]{2,0,1:T(8,128)(2,1)}, bf16[128,4,128]{2,0,1:T(8,128)(2,1)S(1)}, u32[]{:S(2)}) copy-start(bf16[128,4,128]{2,0,1:T(8,128)(2,1)S(1)} %copy.110) | copy-start | bytes 393220
  62.1 4.0 %copy-start.26 = (bf16[128,4,128]{2,0,1:T(8,128)(2,1)S(1)}, bf16[128,4,128]{2,0,1:T(8,128)(2,1)}, u32[]{:S(2)}) copy-start(bf16[128,4,128]{2,0,1:T(8,128)(2,1)} %copy.100) | copy-start | bytes 393220
  62.1 4.0 %copy-start.34 = (bf16[128,4,128]{2,0,1:T(8,128)(2,1)S(1)}, bf16[128,4,128]{2,0,1:T(8,128)(2,1)}, u32[]{:S(2)}) copy-start(bf16[128,4,128]{2,0,1:T(8,128)(2,1)} %copy.99) | copy-start | bytes 393220
  62.3 5.3 %copy-start.40 = (bf16[128,4,128]{2,0,1:T(8,128)(2,1)}, bf16[128,4,128]{2,0,1:T(8,128)(2,1)S(1)}, u32[]{:S(2)}) copy-start(bf16[128,4,128]{2,0,1:T(8,128)(2,1)S(1)} %copy.98) | copy-start | bytes 393220
  63.2 4.6 %copy-start.38 = (bf16[128,4,128]{2,0,1:T(8,128)(2,1)}, bf16[128,4,128]{2,0,1:T(8,128)(2,1)S(1)}, u32[]{:S(2)}) copy-start(bf16[128,4,128]{2,0,1:T(8,128)(2,1)S(1)} %copy.86) | copy-start | bytes 393220
  69.1 90.3 %copy-start.49 = (pred[128]{0:T(512)(128)(4,1)S(1)}, pred[128]{0:T(512)(128)(4,1)}, u32[]{:S(2)}) copy-start(pred[128]{0:T(512)(128)(4,1)} %compare_bitcast_fusion) | copy-start | bytes 388
  165.7 4.4 %copy-start.46 = (bf16[128,512]{0,1:T(8,128)(2,1)S(1)}, bf16[128,512]{0,1:T(8,128)(2,1)}, u32[]{:S(2)}) copy-start(bf16[128,512]{0,1:T(8,128)(2,1)} %get-tuple-element.43) | copy-start | bytes 393220
  170.1 8.0 %copy-start.15 = (bf16[128,4,128]{2,0,1:T(8,128)(2,1)S(1)}, bf16[128,4,128]{2,0,1:T(8,128)(2,1)}, u32[]{:S(2)}) copy-start(bf16[128,4,128]{2,0,1:T(8,128)(2,1)} %copy.103) | copy-start | bytes 393220
  170.1 8.0 %copy-start.19 = (bf16[128,4,128]{2,0,1:T(8,128)(2,1)S(1)}, bf16[128,4,128]{2,0,1:T(8,128)(2,1)}, u32[]{:S(2)}) copy-start(bf16[128,4,128]{2,0,1:T(8,128)(2,1)} %copy.102) | copy-start | bytes 393220
  179.2 8.4 %copy-start.12 = (bf16[128,4,128]{2,0,1:T(8,128)(2,1)S(1)}, bf16[128,4,128]{2,0,1:T(8,128)(2,1)}, u32[]{:S(2)}) copy-start(bf16[128,4,128]{2,0,1:T(8,128)(2,1)} %copy.92) | copy-start | bytes 393220
  179.2 8.4 %copy-start.14 = (bf16[128,4,128]{2,0,1:T(8,128)(2,1)S(1)}, bf16[128,4,128]{2,0,1:T(8,128)(2,1)}, u32[]{:S(2)}) copy-start(bf16[128,4,128]{2,0,1:T(8,128)(2,1)} %copy.91) | copy-start | bytes 393220
  179.3 8.4 %copy-start.18 = (bf16[128,4,128]{2,0,1:T(8,128)(2,1)S(1)}, bf16[128,4,128]{2,0,1:T(8,128)(2,1)}, u32[]{:S(2)}) copy-start(bf16[128,4,128]{2,0,1:T(8,128)(2,1)} %copy.90) | copy-start | bytes 393220
  188.8 7.9 %copy-start.13 = (bf16[128,4,128]{2,0,1:T(8,128)(2,1)S(1)}, bf16[128,4,128]{2,0,1:T(8,128)(2,1)}, u32[]{:S(2)}) copy-start(bf16[128,4,128]{2,0,1:T(8,128)(2,1)} %copy.79) | copy-start | bytes 393220
  188.8 7.9 %copy-start.16 = (bf16[128,4,128]{2,0,1:T(8,128)(2,1)S(1)}, bf16[128,4,128]{2,0,1:T(8,128)(2,1)}, u32[]{:S(2)}) copy-start(bf16[128,4,128]{2,0,1:T(8,128)(2,1)} %copy.78) | copy-start | bytes 393220
  197.8 9.1 %copy-start.20 = (bf16[128,4,128]{0,2,1:T(8,128)(2,1)S(1)}, bf16[128,4,128]{0,2,1:T(8,128)(2,1)}, u32[]{:S(2)}) copy-start(bf16[128,4,128]{0,2,1:T(8,128)(2,1)} %slice.378) | copy-start | bytes 393220
  197.8 9.2 %copy-start.21 = (bf16[128,4,128]{0,2,1:T(8,128)(2,1)S(1)}, bf16[128,4,128]{0,2,1:T(8,128)(2,1)}, u32[]{:S(2)}) copy-start(bf16[128,4,128]{0,2,1:T(8,128)(2,1)} %slice.379) | copy-start | bytes 393220
  216.2 3.9 %copy-start.3 = (f32[384,4,128]{0,2,1:T(8,128)S(1)}, f32[384,4,128]{0,2,1:T(8,128)}, u32[]{:S(2)}) copy-start(f32[384,4,128]{0,2,1:T(8,128)} %convolution_bitcast_fusion.1) | copy-start | bytes 2359300
  218.7 26.6 %collective-permute-start.2 = (bf16[2,128,2048]{2,1,0:T(8,128)(2,1)}, bf16[2,128,2048]{2,1,0:T(8,128)(2,1)}, u32[]{:S(2)}, u32[]{:S(2)}) collective-permute-start(bf16[2,128,2048]{2,1,0:T(8,128)(2,1)} %pad_maximum_fusion), channel_id=1, source_target_pairs={{1,0},{2,1},{3,2},{4,3},{5,4},{6,5},{7,6},{8,7},{9,8},{10,9},{11,1... | collective-permute-start | bytes 3145736 | tf_op jit(solution)/shard_map/ppermute | solution.py:17
  223.5 11.0 %copy-start.29 = (bf16[128,4,128]{2,0,1:T(8,128)(2,1)S(1)}, bf16[128,4,128]{2,0,1:T(8,128)(2,1)}, u32[]{:S(2)}) copy-start(bf16[128,4,128]{2,0,1:T(8,128)(2,1)} %copy.112) | copy-start | bytes 393220
  245.3 4.0 %copy-start.27 = (bf16[128,4,128]{2,0,1:T(8,128)(2,1)S(1)}, bf16[128,4,128]{2,0,1:T(8,128)(2,1)}, u32[]{:S(2)}) copy-start(bf16[128,4,128]{2,0,1:T(8,128)(2,1)} %copy.100) | copy-start | bytes 393220
  245.3 4.0 %copy-start.35 = (bf16[128,4,128]{2,0,1:T(8,128)(2,1)S(1)}, bf16[128,4,128]{2,0,1:T(8,128)(2,1)}, u32[]{:S(2)}) copy-start(bf16[128,4,128]{2,0,1:T(8,128)(2,1)} %copy.99) | copy-start | bytes 393220
  245.3 4.0 %copy-start.41 = (bf16[128,4,128]{2,0,1:T(8,128)(2,1)S(1)}, bf16[128,4,128]{2,0,1:T(8,128)(2,1)}, u32[]{:S(2)}) copy-start(bf16[128,4,128]{2,0,1:T(8,128)(2,1)} %copy-done.40) | copy-start | bytes 393220
  247.9 4.0 %copy-start.43 = (bf16[4,128,128]{2,1,0:T(8,128)(2,1)S(1)}, bf16[4,128,128]{2,1,0:T(8,128)(2,1)}, u32[]{:S(2)}) copy-start(bf16[4,128,128]{2,1,0:T(8,128)(2,1)} %convolution_convert_fusion) | copy-start | bytes 393220
  247.9 5.2 %copy-start.25 = (bf16[128,4,128]{2,0,1:T(8,128)(2,1)S(1)}, bf16[128,4,128]{2,0,1:T(8,128)(2,1)}, u32[]{:S(2)}) copy-start(bf16[128,4,128]{2,0,1:T(8,128)(2,1)} %copy.88) | copy-start | bytes 393220
  247.9 5.2 %copy-start.33 = (bf16[128,4,128]{2,0,1:T(8,128)(2,1)S(1)}, bf16[128,4,128]{2,0,1:T(8,128)(2,1)}, u32[]{:S(2)}) copy-start(bf16[128,4,128]{2,0,1:T(8,128)(2,1)} %copy.87) | copy-start | bytes 393220
  247.9 25.9 %collective-permute-start.3 = (bf16[2,128,2048]{2,1,0:T(8,128)(2,1)}, bf16[2,128,2048]{2,1,0:T(8,128)(2,1)}, u32[]{:S(2)}, u32[]{:S(2)}) collective-permute-start(bf16[2,128,2048]{2,1,0:T(8,128)(2,1)} %fusion.8), channel_id=1, source_target_pairs={{1,0},{2,1},{3,2},{4,3},{5,4},{6,5},{7,6},{8,7},{9,8},{10,9},{11,1... | collective-permute-start | bytes 3145736 | tf_op jit(solution)/shard_map/ppermute | solution.py:17
  253.1 4.3 %copy-start.4 = (f32[128,4,128]{0,2,1:T(8,128)S(1)}, f32[128,4,128]{0,2,1:T(8,128)}, u32[]{:S(2)}) copy-start(f32[128,4,128]{0,2,1:T(8,128)} %get-tuple-element.33) | copy-start | bytes 786436
  (23 other events, 52.3 us)
Sparse Core Ops, SparseCore 0:
  9.8 143.3 all-gather.1
where the time goes:
time: 285 us; the launch traced here: 283 us
  waiting for transfers between devices  124 us (44%)
  local copies, waits for them, and re-layouts  73.7 us (26%)
  matrix products  47.6 us (17%)
  between operations  14.9 us (5%)
  other arithmetic  11.8 us (4%)
  starting transfers between devices  11.6 us (4%)
    all_gather x1, waiting for transfers between devices, shards(): piece = lax.all_gather(out_weight, 'dp', axis=2, tiled=True)  84 us
    ppermute x4, waiting for transfers between devices, passed_along(): lax.ppermute(value, axis, [(source, source + steps) for source in range(f...  39.1 us
    reshape x24, local copies, waits for them, and re-layouts, flatten(): return array.reshape((array.shape[0], array.shape[1] * array.shape[2]))  17 us
    slice x8, local copies, waits for them, and re-layouts, shards(): key_terms[back].append(flatten(grad_k[place * rows:(place + 1) * rows]))  12.4 us
    dot_general x4, matrix products, local_grads(): jnp.einsum('hqk,qhe->khe', dscore, query, preferred_element_type=jnp.floa...  11.6 us
    ppermute x4, starting transfers between devices, passed_along(): lax.ppermute(value, axis, [(source, source + steps) for source in range(f...  11.6 us
    squeeze x12, local copies, waits for them, and re-layouts, shards(): values = jnp.concatenate([item[1] for item in window], axis=0)  11.1 us
    slice x8, local copies, waits for them, and re-layouts, shards(): value_terms[back].append(flatten(grad_v[place * rows:(place + 1) * rows]))  11 us
  transfers between devices with their start and end apart: 5, of which 5 were waited for; matrix products, arithmetic and copies ran while one was open for 22% of the time, Pallas kernels for 0%

commit v1 on v0

v1 whole, which is shorter than its diff:
```python
import jax
import jax.numpy as jnp
from jax import lax
from jax.experimental import pallas as pl
from jax.experimental.pallas import tpu as pltpu
from jax.sharding import PartitionSpec as P

HEAD_DIM = 128
ROWS = 128
WIDTH = 2048
REACH = 2
PART = 512
CHUNK = 256
COUNT = WIDTH // CHUNK
SCALE = HEAD_DIM ** -0.5
NEG = -1e30
F32 = jnp.float32
BF16 = jnp.bfloat16
MESH = pl.DeviceIdType.MESH
LAST = (((1,), (1,)), ((), ()))
FIRST = (((0,), (0,)), ((), ()))


def down(row):
    return jnp.broadcast_to(row.astype(F32), (ROWS, ROWS)).T


def kernel(
    q_ref, kv_ref, gy_ref, tags_ref, seg_ref, w_ref, gq_ref, gkv_ref,
    wg, gyb, tagb, gm, psend, precv, pown, near, far, bias, t1, t0, sa, ra, sb, rb,
    w_sem, s_gy, r_gy, s_tag, r_tag, s_w, r_w, s_p, r_p, s_kv, r_kv,
):
    dp, seq = lax.axis_index("dp"), lax.axis_index("seq")
    x, slot, core = lax.div(dp, 4), lax.rem(dp, 4), lax.rem(dp, 2)
    y_lo = lax.div(slot, 2)
    other = lax.rem(slot + 2, 4)
    after, before = (dp, lax.rem(seq + 1, 16)), (dp, lax.rem(seq + 15, 16))
    beside = dp + 2 - 4 * y_lo
    above = (beside, lax.rem(seq + 8 * y_lo, 16))
    below = (beside, lax.rem(seq + 8 - 8 * y_lo, 16))
    partner = (dp + 1 - 2 * core, seq)
    across = [None] + [(lax.rem(dp + 4 * o, 16), seq) for o in range(1, 4)]

    load = pltpu.make_async_copy(
        w_ref, wg.at[:, :, pl.ds(pl.multiple_of(slot * 128, 128), 128)], w_sem
    )
    load.start()
    barrier = pltpu.get_barrier_semaphore()
    for peer in (after, before, above, below, partner, *across[1:]):
        pl.semaphore_signal(barrier, inc=1, device_id=peer, device_id_type=MESH)
    pl.semaphore_wait(barrier, 8)

    def remote(src, dst, send, recv, to):
        return pltpu.make_async_remote_copy(
            src_ref=src, dst_ref=dst, send_sem=send, recv_sem=recv,
            device_id=to, device_id_type=MESH,
        )

    def cols(c):
        return pl.ds(pl.multiple_of(c * CHUNK, CHUNK), CHUNK)

    def place(number):
        return pl.ds(pl.multiple_of(number * 128, 128), 128)

    def tags_to(o):
        return remote(tags_ref, tagb.at[3 - o], s_tag.at[o - 1], r_tag.at[3 - o], across[o])

    def grad_to(o):
        part = pl.ds(pl.multiple_of(lax.rem(x + o, 4) * PART, PART), PART)
        return remote(gy_ref.at[:, part], gyb.at[3 - o], s_gy.at[o - 1], r_gy.at[3 - o], across[o])

    def weight_to(kind, c):
        piece = wg.at[:, cols(c), place(slot)]
        if kind == 0:
            piece, to = wg.at[0, cols(c), place(slot)], above
        elif kind == 1:
            piece, to = wg.at[1, cols(c), place(slot)], below
        elif kind == 2:
            to = partner
        else:
            piece, to = wg.at[:, cols(c), place(other)], partner
        return remote(piece, piece, s_w.at[kind, c], r_w.at[kind, c], to)

    def partial_to(o, c):
        return remote(
            psend.at[o - 1, :, cols(c)], precv.at[3 - o, :, cols(c)],
            s_p.at[o - 1, c], r_p.at[3 - o, c], across[o],
        )

    def kv_to(kind, c):
        src, dst, to = (
            (kv_ref, near, after), (near, far, after), (sa, ra, before), (sb, rb, before)
        )[kind]
        return remote(
            src.at[:, :, cols(c)], dst.at[:, :, cols(c)], s_kv.at[kind, c], r_kv.at[kind, c], to
        )

    for o in (2, 1, 3):
        tags_to(o).start()
        grad_to(o).start()
    kv_to(0, 0).start()
    kv_to(0, 1).start()
    load.wait()

    @pl.loop(0, COUNT)
    def _(c):
        for kind in (0, 1, 2):
            weight_to(kind, c).start()

    own_row = seg_ref[:, place(seq)]
    for back in range(REACH, -1, -1):
        key_row = seg_ref[:, place(jnp.maximum(seq - back, 0))]
        same = down(key_row) == jnp.broadcast_to(own_row.astype(F32), (ROWS, ROWS))
        if back == 0:
            key = lax.broadcasted_iota(jnp.int32, (ROWS, ROWS), 0)
            query = lax.broadcasted_iota(jnp.int32, (ROWS, ROWS), 1)
            block = jnp.where(jnp.logical_and(same, key <= query), 0.0, NEG)
        else:
            block = jnp.where(same, jnp.where(seq >= back, 0.0, NEG).astype(F32), NEG)
        bias[(REACH - back) * ROWS : (REACH - back + 1) * ROWS, :] = block

    for r in range(4):
        if r > 0:
            tags_to(4 - r).wait_recv()
            grad_to(4 - r).wait_recv()
            text = down(tagb[r - 1]) == 1.0
        else:
            text = down(tags_ref[...]) == 1.0
        for j in range(4):
            if r > 0:
                block = gyb[r - 1, :, j * 128 : (j + 1) * 128]
            else:
                block = gy_ref[:, place(x * 4 + j)]
            block = block.astype(F32)
            rows = slice(r * ROWS, (r + 1) * ROWS)
            gm[rows, j * 128 : (j + 1) * 128] = jnp.where(text, block, 0.0).astype(BF16)
            gm[rows, PART + j * 128 : PART + (j + 1) * 128] = jnp.where(text, 0.0, block).astype(BF16)

    def relay(c):
        weight_to(0, c).wait_recv()
        weight_to(1, c).wait_recv()
        weight_to(3, c).start()

    def project(c):
        weight_to(2, c).wait_recv()
        weight_to(3, c).wait_recv()
        total = lax.dot_general(
            gm[:, :PART], wg[1, cols(c), :], LAST, preferred_element_type=F32
        ) + lax.dot_general(gm[:, PART:], wg[0, cols(c), :], LAST, preferred_element_type=F32)
        pown[:, cols(c)] = total[:ROWS]
        for o in (2, 1, 3):
            psend[o - 1, :, cols(c)] = total[o * ROWS : (o + 1) * ROWS].astype(BF16)
            partial_to(o, c).start()

    def attend(c):
        for o in range(1, 4):
            partial_to(o, c).wait_recv()
        grad_out = pown[:, cols(c)]
        for r in range(3):
            grad_out = grad_out + precv[r, :, cols(c)].astype(F32)
        grad_out = grad_out.astype(BF16)
        kv_to(1, c).wait_recv()
        for h in range(CHUNK // HEAD_DIM):
            here = pl.ds(pl.multiple_of(c * CHUNK + h * HEAD_DIM, HEAD_DIM), HEAD_DIM)
            query = q_ref[:, here]
            grad = grad_out[:, h * HEAD_DIM : (h + 1) * HEAD_DIM]
            keys = jnp.concatenate([far[0, :, here], near[0, :, here], kv_ref[0, :, here]], axis=0)
            values = jnp.concatenate([far[1, :, here], near[1, :, here], kv_ref[1, :, here]], axis=0)
            scores = lax.dot_general(keys, query, LAST, preferred_element_type=F32)
            scores = scores * SCALE + bias[...]
            raised = jnp.exp(scores - jnp.max(scores, axis=0, keepdims=True))
            dprob = lax.dot_general(values, grad, LAST, preferred_element_type=F32)
            share = 1.0 / jnp.sum(raised, axis=0, keepdims=True)
            probs = raised * share
            delta = jnp.sum(probs * dprob, axis=0, keepdims=True)
            dscore = (probs * (dprob - delta) * SCALE).astype(BF16)
            grad_q = lax.dot_general(dscore, keys, FIRST, preferred_element_type=F32)
            gq_ref[:, here] = grad_q.astype(BF16)
            grad_k = jnp.dot(dscore, query, preferred_element_type=F32)
            grad_v = jnp.dot(probs.astype(BF16), grad, preferred_element_type=F32)
            for index, term in ((0, grad_k), (1, grad_v)):
                sa[index, :, here] = term[:ROWS].astype(BF16)
                t1[index, :, here] = term[ROWS : 2 * ROWS]
                t0[index, :, here] = term[2 * ROWS :]
        kv_to(2, c).start()

    def fold(c):
        kv_to(2, c).wait_recv()
        sb[:, :, cols(c)] = (ra[:, :, cols(c)].astype(F32) + t1[:, :, cols(c)]).astype(BF16)
        kv_to(3, c).start()

    def finish(c):
        kv_to(3, c).wait_recv()
        gkv_ref[:, :, cols(c)] = (rb[:, :, cols(c)].astype(F32) + t0[:, :, cols(c)]).astype(BF16)

    relay(0)
    relay(1)
    project(0)

    @pl.loop(0, COUNT + 3)
    def _(i):
        @pl.when(i < COUNT)
        def _():
            kv_to(0, i).wait_recv()
            kv_to(1, i).start()

        @pl.when(i + 2 < COUNT)
        def _():
            kv_to(0, i + 2).start()
            relay(i + 2)

        @pl.when(i + 1 < COUNT)
        def _():
            project(i + 1)

        @pl.when(jnp.logical_and(i >= 1, i <= COUNT))
        def _():
            attend(i - 1)

        @pl.when(jnp.logical_and(i >= 2, i <= COUNT + 1))
        def _():
            fold(i - 2)

        @pl.when(i >= 3)
        def _():
            finish(i - 3)

    for o in range(1, 4):
        tags_to(o).wait_send()
        grad_to(o).wait_send()

    @pl.loop(0, COUNT)
    def _(c):
        for kind in range(4):
            weight_to(kind, c).wait_send()
            kv_to(kind, c).wait_send()
        for o in range(1, 4):
            partial_to(o, c).wait_send()


def shards(query, key_value, grad_y, tags, segments, out_weight):
    vmem = pl.BlockSpec(memory_space=pltpu.VMEM)
    dma = pltpu.SemaphoreType.DMA
    pair = (2, ROWS, WIDTH)
    grad_q, grad_kv = pl.pallas_call(
        kernel,
        out_shape=(
            jax.ShapeDtypeStruct((ROWS, WIDTH), BF16),
            jax.ShapeDtypeStruct(pair, BF16),
        ),
        in_specs=[vmem] * 5 + [pl.BlockSpec(memory_space=pl.ANY)],
        out_specs=(vmem, vmem),
        scratch_shapes=[
            pltpu.VMEM((2, WIDTH, PART), BF16),
            pltpu.VMEM((3, ROWS, PART), BF16),
            pltpu.VMEM((3, 1, ROWS), jnp.int32),
            pltpu.VMEM((4 * ROWS, 2 * PART), BF16),
            pltpu.VMEM((3, ROWS, WIDTH), BF16),
            pltpu.VMEM((3, ROWS, WIDTH), BF16),
            pltpu.VMEM((ROWS, WIDTH), F32),
            pltpu.VMEM(pair, BF16),
            pltpu.VMEM(pair, BF16),
            pltpu.VMEM(((REACH + 1) * ROWS, ROWS), F32),
            pltpu.VMEM(pair, F32),
            pltpu.VMEM(pair, F32),
            pltpu.VMEM(pair, BF16),
            pltpu.VMEM(pair, BF16),
            pltpu.VMEM(pair, BF16),
            pltpu.VMEM(pair, BF16),
            dma,
            dma((3,)), dma((3,)), dma((3,)), dma((3,)),
            dma((4, COUNT)), dma((4, COUNT)),
            dma((3, COUNT)), dma((3, COUNT)),
            dma((4, COUNT)), dma((4, COUNT)),
        ],
        compiler_params=pltpu.CompilerParams(
            collective_id=1, has_side_effects=True, vmem_limit_bytes=48 << 20
        ),
        name="mixed_backward",
    )(query[0], key_value[:, 0], grad_y[0], tags, segments, out_weight)
    return grad_q[None], grad_kv[:, None]


def solution(mesh):
    return jax.shard_map(
        shards,
        mesh=mesh,
        in_specs=(
            P("dp", "seq", None),
            P(None, "dp", "seq", None),
            P("dp", "seq", None),
            P("dp", "seq"),
            P("dp", None),
            P(None, None, "dp"),
        ),
        out_specs=(P("dp", "seq", None), P(None, "dp", "seq", None)),
        check_vma=False,
    )
```

time: 285 us -> 97.6 us (0.34)
  the two profiles are of different devices: /device:TPU:1 before, /device:TPU:224 now
where the time goes in v1:
time: 97.6 us; the launch traced here: 97.3 us
  Pallas kernels  89 us (91%)
  local copies, waits for them, and re-layouts  7.64 us (8%)
    pallas_call x1, Pallas kernels, shards(): pl.pallas_call(kernel, out_shape=(jax.ShapeDtypeStruct((ROWS, WIDTH), BF1...  89 us
    unnamed x14, local copies, waits for them, and re-layouts  7.64 us

profile of v1, /device:TPU:224, one launch (start us, length us, event | category | flops | bytes accessed | tf_op | source)
XLA Modules:
  0.0 97.3 jit_solution(13298882171761941079)
XLA Ops:
  0.6 0.0 copy-start.5
  0.6 0.6 copy-done.5
  1.3 0.0 copy-start
  1.3 1.2 %copy-done = bf16[2,1,128,2048]{3,2,1,0:T(8,128)(2,1)S(1)} copy-done((bf16[2,1,128,2048]{3,2,1,0:T(8,128)(2,1)S(1)}, bf16[2,1,128,2048]{3,2,1,0:T(8,128)(2,1)}, u32[]{:S(2)}) %copy-start) | copy-done | bytes 1048600
  2.5 0.0 copy-start.1
  2.5 1.2 %copy-done.1 = bf16[2,2048,128]{2,1,0:T(8,128)(2,1)S(1)} copy-done((bf16[2,2048,128]{2,1,0:T(8,128)(2,1)S(1)}, bf16[2,2048,128]{2,1,0:T(8,128)(2,1)}, u32[]{:S(2)}) %copy-start.1) | copy-done | bytes 1048600
  3.7 0.0 copy-start.2
  3.7 1.0 %copy-done.2 = bf16[1,128,2048]{2,1,0:T(8,128)(2,1)S(1)} copy-done((bf16[1,128,2048]{2,1,0:T(8,128)(2,1)S(1)}, bf16[1,128,2048]{2,1,0:T(8,128)(2,1)}, u32[]{:S(2)}) %copy-start.2) | copy-done | bytes 524312
  4.8 0.0 copy-start.3
  4.8 1.0 %copy-done.3 = bf16[1,128,2048]{2,1,0:T(8,128)(2,1)S(1)} copy-done((bf16[1,128,2048]{2,1,0:T(8,128)(2,1)S(1)}, bf16[1,128,2048]{2,1,0:T(8,128)(2,1)}, u32[]{:S(2)}) %copy-start.3) | copy-done | bytes 524312
  5.8 0.0 copy-start.4
  5.8 0.7 copy-done.4
  6.5 89.0 %mixed_backward.1 = (bf16[128,2048]{1,0:T(8,128)(2,1)S(1)}, bf16[2,128,2048]{2,1,0:T(8,128)(2,1)S(1)}) custom-call(bf16[128,2048]{1,0:T(8,128)(2,1)S(1)} %bitcast.10, bf16[2,128,2048]{2,1,0:T(8,128)(2,1)S(1)} %bitcast.7, bf16[128,2048]{1,0:T(8,128)(2,1)S(1)} %bitcast.11, s32[1,128]{1,0:T(1,128)S(1)} %copy-done.5, s32[1,2048]{1,0:T(1,128)S(1)} %copy-done.4, ...), custom_call_target="tpu_custom_call" | custom-call | tf_op jit(solution)/shard_map/mixed_backward/pallas_call | solution.py:245
  95.6 0.8 copy.11
  96.4 1.0 copy.12
Async XLA Ops:
  0.6 0.7 copy-start.5
  1.3 1.2 %copy-start = (bf16[2,1,128,2048]{3,2,1,0:T(8,128)(2,1)S(1)}, bf16[2,1,128,2048]{3,2,1,0:T(8,128)(2,1)}, u32[]{:S(2)}) copy-start(bf16[2,1,128,2048]{3,2,1,0:T(8,128)(2,1)} %param.7) | copy-start | bytes 3145732
  2.5 1.2 %copy-start.1 = (bf16[2,2048,128]{2,1,0:T(8,128)(2,1)S(1)}, bf16[2,2048,128]{2,1,0:T(8,128)(2,1)}, u32[]{:S(2)}) copy-start(bf16[2,2048,128]{2,1,0:T(8,128)(2,1)} %w_ref.1) | copy-start | bytes 3145732
  3.7 1.0 %copy-start.2 = (bf16[1,128,2048]{2,1,0:T(8,128)(2,1)S(1)}, bf16[1,128,2048]{2,1,0:T(8,128)(2,1)}, u32[]{:S(2)}) copy-start(bf16[1,128,2048]{2,1,0:T(8,128)(2,1)} %param.6) | copy-start | bytes 1572868
  4.8 1.0 %copy-start.3 = (bf16[1,128,2048]{2,1,0:T(8,128)(2,1)S(1)}, bf16[1,128,2048]{2,1,0:T(8,128)(2,1)}, u32[]{:S(2)}) copy-start(bf16[1,128,2048]{2,1,0:T(8,128)(2,1)} %param.8) | copy-start | bytes 1572868
  5.8 0.7 copy-start.4

commit v2 on v1

v2 whole, which is shorter than its diff:
```python
import jax
import jax.numpy as jnp
from jax import lax
from jax.experimental import pallas as pl
from jax.experimental.pallas import tpu as pltpu
from jax.sharding import PartitionSpec as P

HEAD_DIM = 128
ROWS = 128
WIDTH = 2048
REACH = 2
PART = 512
CHUNK = 256
COUNT = WIDTH // CHUNK
HEADS = WIDTH // HEAD_DIM
LEAD = 4
BACK = 3
HOME = 3
SCALE = HEAD_DIM ** -0.5
NEG = -1e30
F32 = jnp.float32
BF16 = jnp.bfloat16
MESH = pl.DeviceIdType.MESH
LAST = (((1,), (1,)), ((), ()))
FIRST = (((0,), (0,)), ((), ()))


def down(row):
    return jnp.broadcast_to(row.astype(F32), (ROWS, ROWS)).T


def kernel(
    q_in, kv_in, gy_in, tags_in, seg_in, w_in, gq_ref, gkv_ref,
    q_ref, kv_ref, gy_ref, tags_ref, seg_ref, wg, gyb, tagb, gm, psend, precv, pown, near, far, bias, t1, t0, sa, ra, sb, rb,
    in_sem, kv_sem, s_gy, r_gy, s_tag, r_tag, s_w, r_w, s_p, r_p, s_kv, r_kv,
):
    dp, seq = lax.axis_index("dp"), lax.axis_index("seq")
    x, slot, core = lax.div(dp, 4), lax.rem(dp, 4), lax.rem(dp, 2)
    y_lo = lax.div(slot, 2)
    other = lax.rem(slot + 2, 4)
    after, before = (dp, lax.rem(seq + 1, 16)), (dp, lax.rem(seq + 15, 16))
    has_after, has_before = seq < 15, seq > 0
    spreads = lax.div(seq, 8) != lax.div(lax.rem(seq, 8), 4)
    beside = dp + 2 - 4 * y_lo
    above = (beside, lax.rem(seq + 8 * y_lo, 16))
    below = (beside, lax.rem(seq + 8 - 8 * y_lo, 16))
    partner = (dp + 1 - 2 * core, seq)
    across = [None] + [(lax.rem(dp + 4 * o, 16), seq) for o in range(1, 4)]

    def cols(c):
        return pl.ds(pl.multiple_of(c * CHUNK, CHUNK), CHUNK)

    def place(number):
        return pl.ds(pl.multiple_of(number * 128, 128), 128)

    def head(u):
        return pl.ds(pl.multiple_of(u * HEAD_DIM, HEAD_DIM), HEAD_DIM)

    def kv_load(c):
        return pltpu.make_async_copy(kv_in.at[:, :, cols(c)], kv_ref.at[:, :, cols(c)], kv_sem.at[c])

    load_tags = pltpu.make_async_copy(tags_in, tags_ref, in_sem.at[0])
    load_gy = pltpu.make_async_copy(gy_in, gy_ref, in_sem.at[1])
    load_w = pltpu.make_async_copy(w_in, wg.at[:, :, place(slot)], in_sem.at[2])
    load_seg = pltpu.make_async_copy(seg_in, seg_ref, in_sem.at[3])
    load_q = pltpu.make_async_copy(q_in, q_ref, in_sem.at[4])
    load_tags.start()
    load_gy.start()
    for c in range(2):
        kv_load(c).start()
    load_w.start()
    load_seg.start()
    load_q.start()
    for c in range(2, COUNT):
        kv_load(c).start()
    barrier = pltpu.get_barrier_semaphore()
    for peer in (after, before, above, below, partner, *across[1:]):
        pl.semaphore_signal(barrier, inc=1, device_id=peer, device_id_type=MESH)
    pl.semaphore_wait(barrier, 8)

    def remote(src, dst, send, recv, to):
        return pltpu.make_async_remote_copy(
            src_ref=src, dst_ref=dst, send_sem=send, recv_sem=recv,
            device_id=to, device_id_type=MESH,
        )

    def tags_to(o):
        return remote(tags_ref, tagb.at[3 - o], s_tag.at[o - 1], r_tag.at[3 - o], across[o])

    def grad_to(o):
        part = pl.ds(pl.multiple_of(lax.rem(x + o, 4) * PART, PART), PART)
        return remote(gy_ref.at[:, part], gyb.at[3 - o], s_gy.at[o - 1], r_gy.at[3 - o], across[o])

    def weight_to(kind, c):
        piece = wg.at[:, cols(c), place(other if kind == 3 else slot)]
        to = (above, below, partner, partner)[kind]
        return remote(piece, piece, s_w.at[kind], r_w.at[max(kind - 1, 0), c], to)

    def partial_to(o, c):
        return remote(
            psend.at[o - 1, :, cols(c)], precv.at[3 - o, :, cols(c)],
            s_p.at[o - 1], r_p.at[3 - o, c], across[o],
        )

    def kv_to(kind, u):
        src, dst, to = (
            (kv_ref, near, after), (near, far, after), (sa, ra, before), (sb, rb, before)
        )[kind]
        return remote(
            src.at[:, :, head(u)], dst.at[:, :, head(u)], s_kv.at[kind], r_kv.at[kind, u], to
        )

    def send(kind, c):
        pl.when(has_after if kind < 2 else has_before)(lambda: kv_to(kind, c).start())

    def receive(kind, c):
        pl.when(has_before if kind < 2 else has_after)(lambda: kv_to(kind, c).wait_recv())

    load_tags.wait()
    load_gy.wait()
    for o in (2, 1, 3):
        tags_to(o).start()
        grad_to(o).start()
    for c in range(LEAD // 2):
        kv_load(c).wait()
        send(0, 2 * c)
        send(0, 2 * c + 1)
    load_w.wait()

    @pl.loop(0, COUNT)
    def _(c):
        @pl.when(spreads)
        def _():
            weight_to(0, c).start()
            weight_to(1, c).start()

        weight_to(2, c).start()

    @pl.when(jnp.logical_not(has_before))
    def _():
        near[...] = jnp.zeros_like(near)
        far[...] = jnp.zeros_like(far)

    @pl.when(jnp.logical_not(has_after))
    def _():
        ra[...] = jnp.zeros_like(ra)
        rb[...] = jnp.zeros_like(rb)

    load_seg.wait()
    own_row = seg_ref[:, place(seq)]
    for back in range(REACH, -1, -1):
        key_row = seg_ref[:, place(jnp.maximum(seq - back, 0))]
        same = down(key_row) == jnp.broadcast_to(own_row.astype(F32), (ROWS, ROWS))
        if back == 0:
            key = lax.broadcasted_iota(jnp.int32, (ROWS, ROWS), 0)
            query = lax.broadcasted_iota(jnp.int32, (ROWS, ROWS), 1)
            block = jnp.where(jnp.logical_and(same, key <= query), 0.0, NEG)
        else:
            block = jnp.where(same, jnp.where(seq >= back, 0.0, NEG).astype(F32), NEG)
        bias[(REACH - back) * ROWS : (REACH - back + 1) * ROWS, :] = block

    for r in range(4):
        if r > 0:
            tags_to(4 - r).wait_recv()
            grad_to(4 - r).wait_recv()
            text = down(tagb[r - 1]) == 1.0
        else:
            text = down(tags_ref[...]) == 1.0
        for j in range(4):
            if r > 0:
                block = gyb[r - 1, :, j * 128 : (j + 1) * 128]
            else:
                block = gy_ref[:, place(x * 4 + j)]
            block = block.astype(F32)
            rows = slice(r * ROWS, (r + 1) * ROWS)
            gm[rows, j * 128 : (j + 1) * 128] = jnp.where(text, block, 0.0).astype(BF16)
            gm[rows, PART + j * 128 : PART + (j + 1) * 128] = jnp.where(text, 0.0, block).astype(BF16)

    def relay(c):
        weight_to(0, c).wait_recv()
        weight_to(3, c).start()

    def project(c):
        weight_to(2, c).wait_recv()
        weight_to(3, c).wait_recv()
        total = lax.dot_general(
            gm[:, :PART], wg[1, cols(c), :], LAST, preferred_element_type=F32
        ) + lax.dot_general(gm[:, PART:], wg[0, cols(c), :], LAST, preferred_element_type=F32)
        pown[:, cols(c)] = total[:ROWS]
        for o in (2, 1, 3):
            psend[o - 1, :, cols(c)] = total[o * ROWS : (o + 1) * ROWS].astype(BF16)
            partial_to(o, c).start()

    def attend(u, first):
        if first:
            for o in range(1, 4):
                partial_to(o, lax.div(u, 2)).wait_recv()
        here = head(u)
        grad = pown[:, here]
        for r in range(3):
            grad = grad + precv[r, :, here].astype(F32)
        grad = grad.astype(BF16)
        query = q_ref[:, here]
        receive(1, u)
        keys = jnp.concatenate([far[0, :, here], near[0, :, here], kv_ref[0, :, here]], axis=0)
        values = jnp.concatenate([far[1, :, here], near[1, :, here], kv_ref[1, :, here]], axis=0)
        scores = lax.dot_general(keys, query, LAST, preferred_element_type=F32)
        scores = scores * SCALE + bias[...]
        raised = jnp.exp(scores - jnp.max(scores, axis=0, keepdims=True))
        dprob = lax.dot_general(values, grad, LAST, preferred_element_type=F32)
        share = 1.0 / jnp.sum(raised, axis=0, keepdims=True)
        probs = raised * share
        delta = jnp.sum(probs * dprob, axis=0, keepdims=True)
        dscore = (probs * (dprob - delta) * SCALE).astype(BF16)
        grad_k = jnp.dot(dscore, query, preferred_element_type=F32)
        grad_v = jnp.dot(probs.astype(BF16), grad, preferred_element_type=F32)
        sa[0, :, here] = grad_k[:ROWS].astype(BF16)
        sa[1, :, here] = grad_v[:ROWS].astype(BF16)
        send(2, u)
        for index, term in ((0, grad_k), (1, grad_v)):
            t1[index, :, here] = term[ROWS : 2 * ROWS]
            t0[index, :, here] = term[2 * ROWS :]
        grad_q = lax.dot_general(dscore, keys, FIRST, preferred_element_type=F32)
        gq_ref[:, here] = grad_q.astype(BF16)

    def fold(u):
        receive(2, u)
        sb[:, :, head(u)] = (ra[:, :, head(u)].astype(F32) + t1[:, :, head(u)]).astype(BF16)
        send(3, u)

    def finish(u):
        receive(3, u)
        gkv_ref[:, :, head(u)] = (rb[:, :, head(u)].astype(F32) + t0[:, :, head(u)]).astype(BF16)

    def extend(u):
        receive(0, u)
        send(1, u)

    load_q.wait()
    for c in range(LEAD // 2, COUNT):
        kv_load(c).wait()
    relay(0)
    extend(0)
    send(0, LEAD)
    relay(1)
    project(0)

    @pl.loop(0, (HEADS + BACK + HOME + 1) // 2)
    def _(j):
        for b in range(2):
            u = 2 * j + b
            pl.when(jnp.logical_and(u >= 1, u < HEADS))(lambda: extend(u))
            pl.when(jnp.logical_and(u >= 1, u + LEAD < HEADS))(lambda: send(0, u + LEAD))
            if b == 0:
                pl.when(j + 2 < COUNT)(lambda: relay(j + 2))
                pl.when(j + 1 < COUNT)(lambda: project(j + 1))
            pl.when(jnp.logical_and(u >= 1, u <= HEADS))(lambda: attend(u - 1, b == 1))
            pl.when(jnp.logical_and(u >= BACK, u < HEADS + BACK))(lambda: fold(u - BACK))
            last = BACK + HOME
            pl.when(jnp.logical_and(u >= last, u < HEADS + last))(lambda: finish(u - last))

    for o in range(1, 4):
        tags_to(o).wait_send()
        grad_to(o).wait_send()

    whole = wg.at[:, :, place(slot)]
    for kind in range(4):
        done = remote(whole, whole, s_w.at[kind], r_w.at[0, 0], partner)
        if kind < 2:
            pl.when(spreads)(done.wait_send)
        else:
            done.wait_send()
        done = remote(near, far, s_kv.at[kind], r_kv.at[0, 0], after)
        pl.when(has_after if kind < 2 else has_before)(done.wait_send)
    for o in range(1, 4):
        remote(psend.at[o - 1], precv.at[3 - o], s_p.at[o - 1], r_p.at[0, 0], across[o]).wait_send()


def shards(query, key_value, grad_y, tags, segments, out_weight):
    vmem = pl.BlockSpec(memory_space=pltpu.VMEM)
    dma = pltpu.SemaphoreType.DMA
    held = [
        pltpu.with_memory_space_constraint(array, pltpu.HBM)
        for array in (query[0], key_value[:, 0], grad_y[0], tags, segments, out_weight)
    ]
    pair = (2, ROWS, WIDTH)
    grad_q, grad_kv = pl.pallas_call(
        kernel,
        out_shape=(
            jax.ShapeDtypeStruct((ROWS, WIDTH), BF16),
            jax.ShapeDtypeStruct(pair, BF16),
        ),
        in_specs=[pl.BlockSpec(memory_space=pltpu.HBM)] * 6,
        out_specs=(vmem, vmem),
        scratch_shapes=[
            pltpu.VMEM((ROWS, WIDTH), BF16),
            pltpu.VMEM(pair, BF16),
            pltpu.VMEM((ROWS, WIDTH), BF16),
            pltpu.VMEM((1, ROWS), jnp.int32),
            pltpu.VMEM((1, WIDTH), jnp.int32),
            pltpu.VMEM((2, WIDTH, PART), BF16),
            pltpu.VMEM((3, ROWS, PART), BF16),
            pltpu.VMEM((3, 1, ROWS), jnp.int32),
            pltpu.VMEM((4 * ROWS, 2 * PART), BF16),
            pltpu.VMEM((3, ROWS, WIDTH), BF16),
            pltpu.VMEM((3, ROWS, WIDTH), BF16),
            pltpu.VMEM((ROWS, WIDTH), F32),
            pltpu.VMEM(pair, BF16),
            pltpu.VMEM(pair, BF16),
            pltpu.VMEM(((REACH + 1) * ROWS, ROWS), F32),
            pltpu.VMEM(pair, F32),
            pltpu.VMEM(pair, F32),
            pltpu.VMEM(pair, BF16),
            pltpu.VMEM(pair, BF16),
            pltpu.VMEM(pair, BF16),
            pltpu.VMEM(pair, BF16),
            dma((5,)), dma((COUNT,)),
            dma((3,)), dma((3,)), dma((3,)), dma((3,)),
            dma((4,)), dma((3, COUNT)),
            dma((3,)), dma((3, COUNT)),
            dma((4,)), dma((4, HEADS)),
        ],
        compiler_params=pltpu.CompilerParams(
            collective_id=1, has_side_effects=True, vmem_limit_bytes=48 << 20
        ),
        name="mixed_backward",
    )(*held)
    return grad_q[None], grad_kv[:, None]


def solution(mesh):
    return jax.shard_map(
        shards,
        mesh=mesh,
        in_specs=(
            P("dp", "seq", None),
            P(None, "dp", "seq", None),
            P("dp", "seq", None),
            P("dp", "seq"),
            P("dp", None),
            P(None, None, "dp"),
        ),
        out_specs=(P("dp", "seq", None), P(None, "dp", "seq", None)),
        check_vma=False,
    )
```

time: 97.6 us -> 76.2 us (0.78)
  the two profiles are of different devices: /device:TPU:224 before, /device:TPU:24 now
where the time goes in v2:
time: 76.2 us; the launch traced here: 75.6 us
  Pallas kernels  73.2 us (96%)
  local copies, waits for them, and re-layouts  1.77 us (2%)
    pallas_call x1, Pallas kernels, shards(): pl.pallas_call(kernel, out_shape=(jax.ShapeDtypeStruct((ROWS, WIDTH), BF1...  73.2 us
    unnamed x2, local copies, waits for them, and re-layouts  1.77 us

profile of v2, /device:TPU:24, one launch (start us, length us, event | category | flops | bytes accessed | tf_op | source)
XLA Modules:
  0.0 75.6 jit_solution(4022679614597041134)
XLA Ops:
  0.6 73.2 %mixed_backward.1 = (bf16[128,2048]{1,0:T(8,128)(2,1)S(1)}, bf16[2,128,2048]{2,1,0:T(8,128)(2,1)S(1)}) custom-call(bf16[128,2048]{1,0:T(8,128)(2,1)} %bitcast.10, bf16[2,128,2048]{2,1,0:T(8,128)(2,1)} %bitcast.9, bf16[128,2048]{1,0:T(8,128)(2,1)} %bitcast.11, s32[1,128]{1,0:T(1,128)} %tags_in.1, s32[1,2048]{1,0:T(1,128)} %seg_in.1, bf16[2,2048,128]{2,1,0:T(8,128)(2,1)} %w_in.1), custom_call_target="tpu_custom_call" | custom-call | tf_op jit(solution)/shard_map/mixed_backward/pallas_call | solution.py:287
  73.8 0.8 %copy.11 = bf16[1,128,2048]{2,1,0:T(8,128)(2,1)} copy(bf16[1,128,2048]{2,1,0:T(8,128)(2,1)S(1)} %bitcast.8) | data formatting | bytes 1048576
  74.6 1.0 %copy.12 = bf16[2,1,128,2048]{3,2,1,0:T(8,128)(2,1)} copy(bf16[2,1,128,2048]{3,2,1,0:T(8,128)(2,1)S(1)} %bitcast.7) | data formatting | bytes 2097152

commit v3 on v2

--- a/solution.py
+++ b/solution.py
@@ -8,14 +8,14 @@
 HEAD_DIM = 128
 ROWS = 128
 WIDTH = 2048
-REACH = 2
 PART = 512
 CHUNK = 256
 COUNT = WIDTH // CHUNK
 HEADS = WIDTH // HEAD_DIM
-LEAD = 4
-BACK = 3
-HOME = 3
+LEAD = 16
+NEXT = 3
+BACK = 7
+HOME = 12
 SCALE = HEAD_DIM ** -0.5
 NEG = -1e30
 F32 = jnp.float32
@@ -31,7 +31,9 @@
 
 def kernel(
     q_in, kv_in, gy_in, tags_in, seg_in, w_in, gq_ref, gkv_ref,
-    q_ref, kv_ref, gy_ref, tags_ref, seg_ref, wg, gyb, tagb, gm, psend, precv, pown, near, far, bias, t1, t0, sa, ra, sb, rb,
+    q_ref, kv_ref, gy_ref, tags_ref, seg_ref, wg, gyb, tagb, gm, psend, precv, pown, bias,
+    near, q_next, grad_own, grad_next, raised, dprob, up_own, down_own, up_got, down_got,
+    q_part, q_got, q_sum, kv_part, kv_got, kv_sum,
     in_sem, kv_sem, s_gy, r_gy, s_tag, r_tag, s_w, r_w, s_p, r_p, s_kv, r_kv,
 ):
     dp, seq = lax.axis_index("dp"), lax.axis_index("seq")
@@ -102,19 +104,32 @@
             s_p.at[o - 1], r_p.at[3 - o, c], across[o],
         )
 
-    def kv_to(kind, u):
-        src, dst, to = (
-            (kv_ref, near, after), (near, far, after), (sa, ra, before), (sb, rb, before)
-        )[kind]
-        return remote(
-            src.at[:, :, head(u)], dst.at[:, :, head(u)], s_kv.at[kind], r_kv.at[kind, u], to
-        )
+    moves = (
+        (kv_ref, near, after),
+        (q_ref, q_next, before),
+        (grad_own, grad_next, before),
+        (up_own, up_got, before),
+        (down_own, down_got, after),
+        (q_part, q_got, after),
+        (kv_part, kv_got, before),
+    )
+    forward = (True, False, False, False, True, True, False)
+
+    def move(kind, u):
+        src, dst, to = moves[kind]
+        if kind in (3, 4):
+            src, dst = src.at[u], dst.at[u]
+        elif kind in (0, 6):
+            src, dst = src.at[:, :, head(u)], dst.at[:, :, head(u)]
+        else:
+            src, dst = src.at[:, head(u)], dst.at[:, head(u)]
+        return remote(src, dst, s_kv.at[kind], r_kv.at[kind, u], to)
 
     def send(kind, c):
-        pl.when(has_after if kind < 2 else has_before)(lambda: kv_to(kind, c).start())
+        pl.when(has_after if forward[kind] else has_before)(lambda: move(kind, c).start())
 
     def receive(kind, c):
-        pl.when(has_before if kind < 2 else has_after)(lambda: kv_to(kind, c).wait_recv())
+        pl.when(has_before if forward[kind] else has_after)(lambda: move(kind, c).wait_recv())
 
     load_tags.wait()
     load_gy.wait()
@@ -125,6 +140,12 @@
         kv_load(c).wait()
         send(0, 2 * c)
         send(0, 2 * c + 1)
+    load_q.wait()
+
+    @pl.loop(0, HEADS)
+    def _(u):
+        send(1, u)
+
     load_w.wait()
 
     @pl.loop(0, COUNT)
@@ -136,28 +157,35 @@
 
         weight_to(2, c).start()
 
+    first_rows = lax.broadcasted_iota(jnp.int32, (HEADS, 8, ROWS), 1)
+
     @pl.when(jnp.logical_not(has_before))
     def _():
         near[...] = jnp.zeros_like(near)
-        far[...] = jnp.zeros_like(far)
+        q_got[...] = jnp.zeros_like(q_got)
+        down_got[...] = jnp.where(first_rows == 0, NEG, 0.0).astype(F32)
 
     @pl.when(jnp.logical_not(has_after))
     def _():
-        ra[...] = jnp.zeros_like(ra)
-        rb[...] = jnp.zeros_like(rb)
+        q_next[...] = jnp.zeros_like(q_next)
+        grad_next[...] = jnp.zeros_like(grad_next)
+        kv_got[...] = jnp.zeros_like(kv_got)
+        up_got[...] = jnp.ones_like(up_got)
 
     load_seg.wait()
-    own_row = seg_ref[:, place(seq)]
-    for back in range(REACH, -1, -1):
-        key_row = seg_ref[:, place(jnp.maximum(seq - back, 0))]
-        same = down(key_row) == jnp.broadcast_to(own_row.astype(F32), (ROWS, ROWS))
-        if back == 0:
+    behind, ahead = jnp.maximum(seq - 1, 0), jnp.minimum(seq + 1, 15)
+    near_valid = jnp.where(has_before, 0.0, NEG).astype(F32)
+    next_valid = jnp.where(has_after, near_valid, NEG).astype(F32)
+    for part, (key_block, query_block) in enumerate(((behind, ahead), (behind, seq), (seq, seq))):
+        query_row = seg_ref[:, place(query_block)].astype(F32)
+        same = down(seg_ref[:, place(key_block)]) == jnp.broadcast_to(query_row, (ROWS, ROWS))
+        if part == 2:
             key = lax.broadcasted_iota(jnp.int32, (ROWS, ROWS), 0)
             query = lax.broadcasted_iota(jnp.int32, (ROWS, ROWS), 1)
             block = jnp.where(jnp.logical_and(same, key <= query), 0.0, NEG)
         else:
-            block = jnp.where(same, jnp.where(seq >= back, 0.0, NEG).astype(F32), NEG)
-        bias[(REACH - back) * ROWS : (REACH - back + 1) * ROWS, :] = block
+            block = jnp.where(same, (next_valid, near_valid)[part], NEG)
+        bias[part * ROWS : (part + 1) * ROWS, :] = block
 
     for r in range(4):
         if r > 0:
@@ -191,73 +219,115 @@
             psend[o - 1, :, cols(c)] = total[o * ROWS : (o + 1) * ROWS].astype(BF16)
             partial_to(o, c).start()
 
-    def attend(u, first):
+    def collect(u, first):
         if first:
             for o in range(1, 4):
                 partial_to(o, lax.div(u, 2)).wait_recv()
+        grad = pown[:, head(u)]
+        for r in range(3):
+            grad = grad + precv[r, :, head(u)].astype(F32)
+        grad_own[:, head(u)] = grad.astype(BF16)
+        send(2, u)
+
+    row = lax.broadcasted_iota(jnp.int32, (8, ROWS), 0)
+
+    def partial_rows(keys, values, query, grad, mask):
+        scores = lax.dot_general(keys, query, LAST, preferred_element_type=F32) * SCALE + mask
+        top = jnp.max(scores, axis=0, keepdims=True)
+        power = jnp.exp(scores - top)
+        grads = lax.dot_general(values, grad, LAST, preferred_element_type=F32)
+        total = jnp.sum(power, axis=0, keepdims=True)
+        dot = jnp.sum(power * grads, axis=0, keepdims=True)
+        return power, grads, jnp.where(row == 0, top, jnp.where(row == 1, total, dot))
+
+    def score(u):
         here = head(u)
-        grad = pown[:, here]
-        for r in range(3):
-            grad = grad + precv[r, :, here].astype(F32)
-        grad = grad.astype(BF16)
-        query = q_ref[:, here]
-        receive(1, u)
-        keys = jnp.concatenate([far[0, :, here], near[0, :, here], kv_ref[0, :, here]], axis=0)
-        values = jnp.concatenate([far[1, :, here], near[1, :, here], kv_ref[1, :, here]], axis=0)
-        scores = lax.dot_general(keys, query, LAST, preferred_element_type=F32)
-        scores = scores * SCALE + bias[...]
-        raised = jnp.exp(scores - jnp.max(scores, axis=0, keepdims=True))
-        dprob = lax.dot_general(values, grad, LAST, preferred_element_type=F32)
-        share = 1.0 / jnp.sum(raised, axis=0, keepdims=True)
-        probs = raised * share
-        delta = jnp.sum(probs * dprob, axis=0, keepdims=True)
-        dscore = (probs * (dprob - delta) * SCALE).astype(BF16)
-        grad_k = jnp.dot(dscore, query, preferred_element_type=F32)
-        grad_v = jnp.dot(probs.astype(BF16), grad, preferred_element_type=F32)
-        sa[0, :, here] = grad_k[:ROWS].astype(BF16)
-        sa[1, :, here] = grad_v[:ROWS].astype(BF16)
-        send(2, u)
-        for index, term in ((0, grad_k), (1, grad_v)):
-            t1[index, :, here] = term[ROWS : 2 * ROWS]
-            t0[index, :, here] = term[2 * ROWS :]
-        grad_q = lax.dot_general(dscore, keys, FIRST, preferred_element_type=F32)
-        gq_ref[:, here] = grad_q.astype(BF16)
-
-    def fold(u):
-        receive(2, u)
-        sb[:, :, head(u)] = (ra[:, :, head(u)].astype(F32) + t1[:, :, head(u)]).astype(BF16)
+        for kind in (0, 1, 2):
+            receive(kind, u)
+        power, grads, down_own[u] = partial_rows(
+            near[0, :, here], near[1, :, here], q_next[:, here], grad_next[:, here], bias[:ROWS]
+        )
+        send(4, u)
+        raised[u, :ROWS], dprob[u, :ROWS] = power, grads
+        power, grads, up_own[u] = partial_rows(
+            jnp.concatenate([near[0, :, here], kv_ref[0, :, here]], axis=0),
+            jnp.concatenate([near[1, :, here], kv_ref[1, :, here]], axis=0),
+            q_ref[:, here], grad_own[:, here], bias[ROWS:],
+        )
         send(3, u)
+        raised[u, ROWS:], dprob[u, ROWS:] = power, grads
+
+    def merge(mine, got, u):
+        top, total, dot = (mine[u, r : r + 1, :] for r in range(3))
+        top_got, total_got, dot_got = (got[u, r : r + 1, :] for r in range(3))
+        both = jnp.maximum(top, top_got)
+        weight, weight_got = jnp.exp(top - both), jnp.exp(top_got - both)
+        share = 1.0 / (total * weight + total_got * weight_got)
+        return weight * share, (dot * weight + dot_got * weight_got) * share
+
+    def grads(u):
+        here = head(u)
+        receive(3, u)
+        receive(4, u)
+        factor, delta = merge(down_own, up_got, u)
+        probs = raised[u, :ROWS] * factor
+        dscore_next = (probs * (dprob[u, :ROWS] - delta) * SCALE).astype(BF16)
+        probs_next = probs.astype(BF16)
+        key_near = near[0, :, here]
+        q_part[:, here] = lax.dot_general(
+            dscore_next, key_near, FIRST, preferred_element_type=F32
+        ).astype(BF16)
+        send(5, u)
+        factor, delta = merge(up_own, down_got, u)
+        probs = raised[u, ROWS:] * factor
+        dscore = (probs * (dprob[u, ROWS:] - delta) * SCALE).astype(BF16)
+        probs = probs.astype(BF16)
+        query, grad = q_ref[:, here], grad_own[:, here]
+        kv_part[0, :, here] = jnp.dot(
+            jnp.concatenate([dscore[:ROWS], dscore_next], axis=1),
+            jnp.concatenate([query, q_next[:, here]], axis=0),
+            preferred_element_type=F32,
+        ).astype(BF16)
+        kv_part[1, :, here] = jnp.dot(
+            jnp.concatenate([probs[:ROWS], probs_next], axis=1),
+            jnp.concatenate([grad, grad_next[:, here]], axis=0),
+            preferred_element_type=F32,
+        ).astype(BF16)
+        send(6, u)
+        kv_sum[0, :, here] = jnp.dot(dscore[ROWS:], query, preferred_element_type=F32)
+        kv_sum[1, :, here] = jnp.dot(probs[ROWS:], grad, preferred_element_type=F32)
+        q_sum[:, here] = lax.dot_general(
+            dscore, jnp.concatenate([key_near, kv_ref[0, :, here]], axis=0), FIRST,
+            preferred_element_type=F32,
+        )
 
     def finish(u):
-        receive(3, u)
-        gkv_ref[:, :, head(u)] = (rb[:, :, head(u)].astype(F32) + t0[:, :, head(u)]).astype(BF16)
-
-    def extend(u):
-        receive(0, u)
-        send(1, u)
-
-    load_q.wait()
+        here = head(u)
+        receive(5, u)
+        gq_ref[:, here] = (q_got[:, here].astype(F32) + q_sum[:, here]).astype(BF16)
+        receive(6, u)
+        gkv_ref[:, :, here] = (kv_got[:, :, here].astype(F32) + kv_sum[:, :, here]).astype(BF16)
+
     for c in range(LEAD // 2, COUNT):
         kv_load(c).wait()
     relay(0)
-    extend(0)
-    send(0, LEAD)
+    project(0)
     relay(1)
-    project(0)
-
-    @pl.loop(0, (HEADS + BACK + HOME + 1) // 2)
+    project(1)
+    relay(2)
+
+    @pl.loop(0, (HEADS + HOME + 1) // 2)
     def _(j):
         for b in range(2):
             u = 2 * j + b
-            pl.when(jnp.logical_and(u >= 1, u < HEADS))(lambda: extend(u))
-            pl.when(jnp.logical_and(u >= 1, u + LEAD < HEADS))(lambda: send(0, u + LEAD))
+            pl.when(u + LEAD < HEADS)(lambda: send(0, u + LEAD))
+            pl.when(u < HEADS)(lambda: collect(u, b == 0))
             if b == 0:
-                pl.when(j + 2 < COUNT)(lambda: relay(j + 2))
-                pl.when(j + 1 < COUNT)(lambda: project(j + 1))
-            pl.when(jnp.logical_and(u >= 1, u <= HEADS))(lambda: attend(u - 1, b == 1))
-            pl.when(jnp.logical_and(u >= BACK, u < HEADS + BACK))(lambda: fold(u - BACK))
-            last = BACK + HOME
-            pl.when(jnp.logical_and(u >= last, u < HEADS + last))(lambda: finish(u - last))
+                pl.when(j + 3 < COUNT)(lambda: relay(j + 3))
+                pl.when(j + 2 < COUNT)(lambda: project(j + 2))
+            pl.when(jnp.logical_and(u >= NEXT, u < HEADS + NEXT))(lambda: score(u - NEXT))
+            pl.when(jnp.logical_and(u >= BACK, u < HEADS + BACK))(lambda: grads(u - BACK))
+            pl.when(jnp.logical_and(u >= HOME, u < HEADS + HOME))(lambda: finish(u - HOME))
 
     for o in range(1, 4):
         tags_to(o).wait_send()
@@ -270,8 +340,9 @@
             pl.when(spreads)(done.wait_send)
         else:
             done.wait_send()
-        done = remote(near, far, s_kv.at[kind], r_kv.at[0, 0], after)
-        pl.when(has_after if kind < 2 else has_before)(done.wait_send)
+    for kind, (src, dst, to) in enumerate(moves):
+        done = remote(src, dst, s_kv.at[kind], r_kv.at[0, 0], to)
+        pl.when(has_after if forward[kind] else has_before)(done.wait_send)
     for o in range(1, 4):
         remote(psend.at[o - 1], precv.at[3 - o], s_p.at[o - 1], r_p.at[0, 0], across[o]).wait_send()
 
@@ -305,20 +376,25 @@
             pltpu.VMEM((3, ROWS, WIDTH), BF16),
             pltpu.VMEM((3, ROWS, WIDTH), BF16),
             pltpu.VMEM((ROWS, WIDTH), F32),
+            pltpu.VMEM((3 * ROWS, ROWS), F32),
+            pltpu.VMEM(pair, BF16),
+            pltpu.VMEM((ROWS, WIDTH), BF16),
+            pltpu.VMEM((ROWS, WIDTH), BF16),
+            pltpu.VMEM((ROWS, WIDTH), BF16),
+            pltpu.VMEM((HEADS, 3 * ROWS, ROWS), F32),
+            pltpu.VMEM((HEADS, 3 * ROWS, ROWS), F32),
+            *[pltpu.VMEM((HEADS, 8, ROWS), F32)] * 4,
+            pltpu.VMEM((ROWS, WIDTH), BF16),
+            pltpu.VMEM((ROWS, WIDTH), BF16),
+            pltpu.VMEM((ROWS, WIDTH), F32),
             pltpu.VMEM(pair, BF16),
             pltpu.VMEM(pair, BF16),
-            pltpu.VMEM(((REACH + 1) * ROWS, ROWS), F32),
             pltpu.VMEM(pair, F32),
-            pltpu.VMEM(pair, F32),
-            pltpu.VMEM(pair, BF16),
-            pltpu.VMEM(pair, BF16),
-            pltpu.VMEM(pair, BF16),
-            pltpu.VMEM(pair, BF16),
             dma((5,)), dma((COUNT,)),
             dma((3,)), dma((3,)), dma((3,)), dma((3,)),
             dma((4,)), dma((3, COUNT)),
             dma((3,)), dma((3, COUNT)),
-            dma((4,)), dma((4, HEADS)),
+            dma((7,)), dma((7, HEADS)),
         ],
         compiler_params=pltpu.CompilerParams(
             collective_id=1, has_side_effects=True, vmem_limit_bytes=48 << 20

time: 76.2 us -> 69 us (0.906)
  Pallas kernels: 73.2 us -> 66.1 us
    pallas_call x1, Pallas kernels: 73.2 us -> 66.1 us  [shards(): pl.pallas_call(kernel, out_shape=(jax.ShapeDtypeStruct((ROWS, WIDTH), BF1...]
where the time goes in v3:
time: 69 us; the launch traced here: 68.5 us
  Pallas kernels  66.1 us (96%)
  local copies, waits for them, and re-layouts  1.77 us (3%)
    pallas_call x1, Pallas kernels, shards(): pl.pallas_call(kernel, out_shape=(jax.ShapeDtypeStruct((ROWS, WIDTH), BF1...  66.1 us
    unnamed x2, local copies, waits for them, and re-layouts  1.77 us

profile of v3, /device:TPU:24, one launch (start us, length us, event | category | flops | bytes accessed | tf_op | source)
XLA Modules:
  0.0 68.5 jit_solution(11073332214265819802)
XLA Ops:
  0.6 66.1 %mixed_backward.1 = (bf16[128,2048]{1,0:T(8,128)(2,1)S(1)}, bf16[2,128,2048]{2,1,0:T(8,128)(2,1)S(1)}) custom-call(bf16[128,2048]{1,0:T(8,128)(2,1)} %bitcast.10, bf16[2,128,2048]{2,1,0:T(8,128)(2,1)} %bitcast.9, bf16[128,2048]{1,0:T(8,128)(2,1)} %bitcast.11, s32[1,128]{1,0:T(1,128)} %tags_in.1, s32[1,2048]{1,0:T(1,128)} %seg_in.1, bf16[2,2048,128]{2,1,0:T(8,128)(2,1)} %w_in.1), custom_call_target="tpu_custom_call" | custom-call | tf_op jit(solution)/shard_map/mixed_backward/pallas_call | solution.py:358
  66.7 0.8 %copy.11 = bf16[1,128,2048]{2,1,0:T(8,128)(2,1)} copy(bf16[1,128,2048]{2,1,0:T(8,128)(2,1)S(1)} %bitcast.8) | data formatting | bytes 1048576
  67.5 1.0 %copy.12 = bf16[2,1,128,2048]{3,2,1,0:T(8,128)(2,1)} copy(bf16[2,1,128,2048]{3,2,1,0:T(8,128)(2,1)S(1)} %bitcast.7) | data formatting | bytes 2097152

commit v4 on v3

--- a/solution.py
+++ b/solution.py
@@ -12,10 +12,11 @@
 CHUNK = 256
 COUNT = WIDTH // CHUNK
 HEADS = WIDTH // HEAD_DIM
-LEAD = 16
+LEAD = 8
+EARLY = 6
 NEXT = 3
 BACK = 7
-HOME = 12
+HOME = 11
 SCALE = HEAD_DIM ** -0.5
 NEG = -1e30
 F32 = jnp.float32
@@ -33,7 +34,7 @@
     q_in, kv_in, gy_in, tags_in, seg_in, w_in, gq_ref, gkv_ref,
     q_ref, kv_ref, gy_ref, tags_ref, seg_ref, wg, gyb, tagb, gm, psend, precv, pown, bias,
     near, q_next, grad_own, grad_next, raised, dprob, up_own, down_own, up_got, down_got,
-    q_part, q_got, q_sum, kv_part, kv_got, kv_sum,
+    up_delta, down_delta, up_delta_got, down_delta_got, q_part, q_got, q_sum, kv_part, kv_got, kv_sum,
     in_sem, kv_sem, s_gy, r_gy, s_tag, r_tag, s_w, r_w, s_p, r_p, s_kv, r_kv,
 ):
     dp, seq = lax.axis_index("dp"), lax.axis_index("seq")
@@ -98,10 +99,10 @@
         to = (above, below, partner, partner)[kind]
         return remote(piece, piece, s_w.at[kind], r_w.at[max(kind - 1, 0), c], to)
 
-    def partial_to(o, c):
+    def partial_to(o, u):
         return remote(
-            psend.at[o - 1, :, cols(c)], precv.at[3 - o, :, cols(c)],
-            s_p.at[o - 1], r_p.at[3 - o, c], across[o],
+            psend.at[o - 1, :, head(u)], precv.at[3 - o, :, head(u)],
+            s_p.at[o - 1], r_p.at[3 - o, u], across[o],
         )
 
     moves = (
@@ -111,15 +112,18 @@
         (up_own, up_got, before),
         (down_own, down_got, after),
         (q_part, q_got, after),
-        (kv_part, kv_got, before),
+        (kv_part.at[1], kv_got.at[1], before),
+        (kv_part.at[0], kv_got.at[0], before),
+        (up_delta, up_delta_got, before),
+        (down_delta, down_delta_got, after),
     )
-    forward = (True, False, False, False, True, True, False)
+    forward = (True, False, False, False, True, True, False, False, False, True)
 
     def move(kind, u):
         src, dst, to = moves[kind]
-        if kind in (3, 4):
+        if kind in (3, 4, 8, 9):
             src, dst = src.at[u], dst.at[u]
-        elif kind in (0, 6):
+        elif kind == 0:
             src, dst = src.at[:, :, head(u)], dst.at[:, :, head(u)]
         else:
             src, dst = src.at[:, head(u)], dst.at[:, head(u)]
@@ -157,13 +161,14 @@
 
         weight_to(2, c).start()
 
-    first_rows = lax.broadcasted_iota(jnp.int32, (HEADS, 8, ROWS), 1)
+    first_rows = lax.broadcasted_iota(jnp.int32, (HEADS, 2, ROWS), 1)
 
     @pl.when(jnp.logical_not(has_before))
     def _():
         near[...] = jnp.zeros_like(near)
         q_got[...] = jnp.zeros_like(q_got)
         down_got[...] = jnp.where(first_rows == 0, NEG, 0.0).astype(F32)
+        down_delta_got[...] = jnp.zeros_like(down_delta_got)
 
     @pl.when(jnp.logical_not(has_after))
     def _():
@@ -171,6 +176,7 @@
         grad_next[...] = jnp.zeros_like(grad_next)
         kv_got[...] = jnp.zeros_like(kv_got)
         up_got[...] = jnp.ones_like(up_got)
+        up_delta_got[...] = jnp.zeros_like(up_delta_got)
 
     load_seg.wait()
     behind, ahead = jnp.maximum(seq - 1, 0), jnp.minimum(seq + 1, 15)
@@ -187,6 +193,124 @@
             block = jnp.where(same, (next_valid, near_valid)[part], NEG)
         bias[part * ROWS : (part + 1) * ROWS, :] = block
 
+    def relay(c):
+        weight_to(0, c).wait_recv()
+        weight_to(3, c).start()
+
+    def project(c):
+        weight_to(2, c).wait_recv()
+        weight_to(3, c).wait_recv()
+        total = lax.dot_general(
+            gm[:, :PART], wg[1, cols(c), :], LAST, preferred_element_type=F32
+        ) + lax.dot_general(gm[:, PART:], wg[0, cols(c), :], LAST, preferred_element_type=F32)
+        pown[:, cols(c)] = total[:ROWS]
+        for o in (2, 1, 3):
+            psend[o - 1, :, cols(c)] = total[o * ROWS : (o + 1) * ROWS].astype(BF16)
+        for h in range(2):
+            for o in (2, 1, 3):
+                partial_to(o, 2 * c + h).start()
+
+    def collect(u):
+        for o in range(1, 4):
+            partial_to(o, u).wait_recv()
+        grad = pown[:, head(u)]
+        for r in range(3):
+            grad = grad + precv[r, :, head(u)].astype(F32)
+        grad_own[:, head(u)] = grad.astype(BF16)
+        send(2, u)
+
+    row = lax.broadcasted_iota(jnp.int32, (2, ROWS), 0)
+
+    def partial_rows(keys, query, mask):
+        scores = lax.dot_general(keys, query, LAST, preferred_element_type=F32) * SCALE + mask
+        top = jnp.max(scores, axis=0, keepdims=True)
+        power = jnp.exp(scores - top)
+        return power, jnp.where(row == 0, top, jnp.sum(power, axis=0, keepdims=True))
+
+    def score(u):
+        here = head(u)
+        receive(0, u)
+        pl.when(u + LEAD < HEADS)(lambda: send(0, u + LEAD))
+        receive(1, u)
+        raised[u, :ROWS], down_own[u] = partial_rows(near[0, :, here], q_next[:, here], bias[:ROWS])
+        send(4, u)
+        keys = jnp.concatenate([near[0, :, here], kv_ref[0, :, here]], axis=0)
+        raised[u, ROWS:], up_own[u] = partial_rows(keys, q_ref[:, here], bias[ROWS:])
+        send(3, u)
+
+    def merge(mine, got, u):
+        top, total = (mine[u, r : r + 1, :] for r in range(2))
+        top_got, total_got = (got[u, r : r + 1, :] for r in range(2))
+        both = jnp.maximum(top, top_got)
+        weight, weight_got = jnp.exp(top - both), jnp.exp(top_got - both)
+        return weight / (total * weight + total_got * weight_got)
+
+    def weigh(u):
+        here = head(u)
+        for kind in (2, 3, 4):
+            receive(kind, u)
+        grad, grad_ahead = grad_own[:, here], grad_next[:, here]
+        value_near, value_own = near[1, :, here], kv_ref[1, :, here]
+        ahead_grads = lax.dot_general(value_near, grad_ahead, LAST, preferred_element_type=F32)
+        ahead_probs = raised[u, :ROWS] * merge(down_own, up_got, u)
+        total = jnp.sum(ahead_probs * ahead_grads, axis=0, keepdims=True)
+        down_delta[u] = total
+        send(9, u)
+        values = jnp.concatenate([value_near, value_own], axis=0)
+        grads = lax.dot_general(values, grad, LAST, preferred_element_type=F32)
+        probs = raised[u, ROWS:] * merge(up_own, down_got, u)
+        up_delta[u] = jnp.sum(probs * grads, axis=0, keepdims=True)
+        send(8, u)
+        raised[u, :ROWS], raised[u, ROWS:] = ahead_probs, probs
+        dprob[u, :ROWS], dprob[u, ROWS:] = ahead_grads, grads
+        probs = probs.astype(BF16)
+        kv_part[1, :, here] = jnp.dot(
+            jnp.concatenate([probs[:ROWS], ahead_probs.astype(BF16)], axis=1),
+            jnp.concatenate([grad, grad_ahead], axis=0),
+            preferred_element_type=F32,
+        ).astype(BF16)
+        send(6, u)
+        kv_sum[1, :, here] = jnp.dot(probs[ROWS:], grad, preferred_element_type=F32)
+
+    def grads(u):
+        here = head(u)
+        receive(8, u)
+        receive(9, u)
+        delta = down_delta[u] + up_delta_got[u]
+        ahead = (raised[u, :ROWS] * (dprob[u, :ROWS] - delta) * SCALE).astype(BF16)
+        query, key_near = q_ref[:, here], near[0, :, here]
+        q_part[:, here] = lax.dot_general(
+            ahead, key_near, FIRST, preferred_element_type=F32
+        ).astype(BF16)
+        send(5, u)
+        delta = up_delta[u] + down_delta_got[u]
+        dscore = (raised[u, ROWS:] * (dprob[u, ROWS:] - delta) * SCALE).astype(BF16)
+        kv_part[0, :, here] = jnp.dot(
+            jnp.concatenate([dscore[:ROWS], ahead], axis=1),
+            jnp.concatenate([query, q_next[:, here]], axis=0),
+            preferred_element_type=F32,
+        ).astype(BF16)
+        send(7, u)
+        kv_sum[0, :, here] = jnp.dot(dscore[ROWS:], query, preferred_element_type=F32)
+        q_sum[:, here] = lax.dot_general(
+            dscore, jnp.concatenate([key_near, kv_ref[0, :, here]], axis=0), FIRST,
+            preferred_element_type=F32,
+        )
+
+    def finish(u):
+        here = head(u)
+        receive(5, u)
+        gq_ref[:, here] = (q_got[:, here].astype(F32) + q_sum[:, here]).astype(BF16)
+        receive(6, u)
+        receive(7, u)
+        gkv_ref[:, :, here] = (kv_got[:, :, here].astype(F32) + kv_sum[:, :, here]).astype(BF16)
+
+    def early(begin, end):
+        pl.loop(begin, end)(score)
+
+    for c in range(LEAD // 2, COUNT):
+        kv_load(c).wait()
+    early(0, 2)
     for r in range(4):
         if r > 0:
             tags_to(4 - r).wait_recv()
@@ -204,129 +328,26 @@
             gm[rows, j * 128 : (j + 1) * 128] = jnp.where(text, block, 0.0).astype(BF16)
             gm[rows, PART + j * 128 : PART + (j + 1) * 128] = jnp.where(text, 0.0, block).astype(BF16)
 
-    def relay(c):
-        weight_to(0, c).wait_recv()
-        weight_to(3, c).start()
-
-    def project(c):
-        weight_to(2, c).wait_recv()
-        weight_to(3, c).wait_recv()
-        total = lax.dot_general(
-            gm[:, :PART], wg[1, cols(c), :], LAST, preferred_element_type=F32
-        ) + lax.dot_general(gm[:, PART:], wg[0, cols(c), :], LAST, preferred_element_type=F32)
-        pown[:, cols(c)] = total[:ROWS]
-        for o in (2, 1, 3):
-            psend[o - 1, :, cols(c)] = total[o * ROWS : (o + 1) * ROWS].astype(BF16)
-            partial_to(o, c).start()
-
-    def collect(u, first):
-        if first:
-            for o in range(1, 4):
-                partial_to(o, lax.div(u, 2)).wait_recv()
-        grad = pown[:, head(u)]
-        for r in range(3):
-            grad = grad + precv[r, :, head(u)].astype(F32)
-        grad_own[:, head(u)] = grad.astype(BF16)
-        send(2, u)
-
-    row = lax.broadcasted_iota(jnp.int32, (8, ROWS), 0)
-
-    def partial_rows(keys, values, query, grad, mask):
-        scores = lax.dot_general(keys, query, LAST, preferred_element_type=F32) * SCALE + mask
-        top = jnp.max(scores, axis=0, keepdims=True)
-        power = jnp.exp(scores - top)
-        grads = lax.dot_general(values, grad, LAST, preferred_element_type=F32)
-        total = jnp.sum(power, axis=0, keepdims=True)
-        dot = jnp.sum(power * grads, axis=0, keepdims=True)
-        return power, grads, jnp.where(row == 0, top, jnp.where(row == 1, total, dot))
-
-    def score(u):
-        here = head(u)
-        for kind in (0, 1, 2):
-            receive(kind, u)
-        power, grads, down_own[u] = partial_rows(
-            near[0, :, here], near[1, :, here], q_next[:, here], grad_next[:, here], bias[:ROWS]
-        )
-        send(4, u)
-        raised[u, :ROWS], dprob[u, :ROWS] = power, grads
-        power, grads, up_own[u] = partial_rows(
-            jnp.concatenate([near[0, :, here], kv_ref[0, :, here]], axis=0),
-            jnp.concatenate([near[1, :, here], kv_ref[1, :, here]], axis=0),
-            q_ref[:, here], grad_own[:, here], bias[ROWS:],
-        )
-        send(3, u)
-        raised[u, ROWS:], dprob[u, ROWS:] = power, grads
-
-    def merge(mine, got, u):
-        top, total, dot = (mine[u, r : r + 1, :] for r in range(3))
-        top_got, total_got, dot_got = (got[u, r : r + 1, :] for r in range(3))
-        both = jnp.maximum(top, top_got)
-        weight, weight_got = jnp.exp(top - both), jnp.exp(top_got - both)
-        share = 1.0 / (total * weight + total_got * weight_got)
-        return weight * share, (dot * weight + dot_got * weight_got) * share
-
-    def grads(u):
-        here = head(u)
-        receive(3, u)
-        receive(4, u)
-        factor, delta = merge(down_own, up_got, u)
-        probs = raised[u, :ROWS] * factor
-        dscore_next = (probs * (dprob[u, :ROWS] - delta) * SCALE).astype(BF16)
-        probs_next = probs.astype(BF16)
-        key_near = near[0, :, here]
-        q_part[:, here] = lax.dot_general(
-            dscore_next, key_near, FIRST, preferred_element_type=F32
-        ).astype(BF16)
-        send(5, u)
-        factor, delta = merge(up_own, down_got, u)
-        probs = raised[u, ROWS:] * factor
-        dscore = (probs * (dprob[u, ROWS:] - delta) * SCALE).astype(BF16)
-        probs = probs.astype(BF16)
-        query, grad = q_ref[:, here], grad_own[:, here]
-        kv_part[0, :, here] = jnp.dot(
-            jnp.concatenate([dscore[:ROWS], dscore_next], axis=1),
-            jnp.concatenate([query, q_next[:, here]], axis=0),
-            preferred_element_type=F32,
-        ).astype(BF16)
-        kv_part[1, :, here] = jnp.dot(
-            jnp.concatenate([probs[:ROWS], probs_next], axis=1),
-            jnp.concatenate([grad, grad_next[:, here]], axis=0),
-            preferred_element_type=F32,
-        ).astype(BF16)
-        send(6, u)
-        kv_sum[0, :, here] = jnp.dot(dscore[ROWS:], query, preferred_element_type=F32)
-        kv_sum[1, :, here] = jnp.dot(probs[ROWS:], grad, preferred_element_type=F32)
-        q_sum[:, here] = lax.dot_general(
-            dscore, jnp.concatenate([key_near, kv_ref[0, :, here]], axis=0), FIRST,
-            preferred_element_type=F32,
-        )
-
-    def finish(u):
-        here = head(u)
-        receive(5, u)
-        gq_ref[:, here] = (q_got[:, here].astype(F32) + q_sum[:, here]).astype(BF16)
-        receive(6, u)
-        gkv_ref[:, :, here] = (kv_got[:, :, here].astype(F32) + kv_sum[:, :, here]).astype(BF16)
-
-    for c in range(LEAD // 2, COUNT):
-        kv_load(c).wait()
     relay(0)
     project(0)
+    early(2, 4)
     relay(1)
     project(1)
+    early(4, EARLY)
     relay(2)
 
     @pl.loop(0, (HEADS + HOME + 1) // 2)
     def _(j):
         for b in range(2):
             u = 2 * j + b
-            pl.when(u + LEAD < HEADS)(lambda: send(0, u + LEAD))
-            pl.when(u < HEADS)(lambda: collect(u, b == 0))
+            pl.when(u < HEADS)(lambda: collect(u))
+            pl.when(u + EARLY < HEADS)(lambda: score(u + EARLY))
+            pl.when(jnp.logical_and(u >= NEXT, u < HEADS + NEXT))(lambda: weigh(u - NEXT))
+            pl.when(jnp.logical_and(u >= BACK, u < HEADS + BACK))(lambda: grads(u - BACK))
             if b == 0:
+                pl.when(j + 2 < COUNT)(lambda: project(j + 2))
+            else:
                 pl.when(j + 3 < COUNT)(lambda: relay(j + 3))
-                pl.when(j + 2 < COUNT)(lambda: project(j + 2))
-            pl.when(jnp.logical_and(u >= NEXT, u < HEADS + NEXT))(lambda: score(u - NEXT))
-            pl.when(jnp.logical_and(u >= BACK, u < HEADS + BACK))(lambda: grads(u - BACK))
             pl.when(jnp.logical_and(u >= HOME, u < HEADS + HOME))(lambda: finish(u - HOME))
 
     for o in range(1, 4):
@@ -383,7 +404,8 @@
             pltpu.VMEM((ROWS, WIDTH), BF16),
             pltpu.VMEM((HEADS, 3 * ROWS, ROWS), F32),
             pltpu.VMEM((HEADS, 3 * ROWS, ROWS), F32),
-            *[pltpu.VMEM((HEADS, 8, ROWS), F32)] * 4,
+            *[pltpu.VMEM((HEADS, 2, ROWS), F32)] * 4,
+            *[pltpu.VMEM((HEADS, 1, ROWS), F32)] * 4,
             pltpu.VMEM((ROWS, WIDTH), BF16),
             pltpu.VMEM((ROWS, WIDTH), BF16),
             pltpu.VMEM((ROWS, WIDTH), F32),
@@ -393,8 +415,8 @@
             dma((5,)), dma((COUNT,)),
             dma((3,)), dma((3,)), dma((3,)), dma((3,)),
             dma((4,)), dma((3, COUNT)),
-            dma((3,)), dma((3, COUNT)),
-            dma((7,)), dma((7, HEADS)),
+            dma((3,)), dma((3, HEADS)),
+            dma((10,)), dma((10, HEADS)),
         ],
         compiler_params=pltpu.CompilerParams(
             collective_id=1, has_side_effects=True, vmem_limit_bytes=48 << 20

time: 69 us -> 68 us (0.986)
  no operation moved by 1% of the time
where the time goes in v4:
time: 68 us; the launch traced here: 67.9 us
  Pallas kernels  65.5 us (96%)
  local copies, waits for them, and re-layouts  1.77 us (3%)
    pallas_call x1, Pallas kernels, shards(): pl.pallas_call(kernel, out_shape=(jax.ShapeDtypeStruct((ROWS, WIDTH), BF1...  65.5 us
    unnamed x2, local copies, waits for them, and re-layouts  1.77 us

profile of v4, /device:TPU:24, one launch (start us, length us, event | category | flops | bytes accessed | tf_op | source)
XLA Modules:
  0.0 67.9 jit_solution(7474635737277345792)
XLA Ops:
  0.6 65.5 %mixed_backward.1 = (bf16[128,2048]{1,0:T(8,128)(2,1)S(1)}, bf16[2,128,2048]{2,1,0:T(8,128)(2,1)S(1)}) custom-call(bf16[128,2048]{1,0:T(8,128)(2,1)} %bitcast.10, bf16[2,128,2048]{2,1,0:T(8,128)(2,1)} %bitcast.9, bf16[128,2048]{1,0:T(8,128)(2,1)} %bitcast.11, s32[1,128]{1,0:T(1,128)} %tags_in.1, s32[1,2048]{1,0:T(1,128)} %seg_in.1, bf16[2,2048,128]{2,1,0:T(8,128)(2,1)} %w_in.1), custom_call_target="tpu_custom_call" | custom-call | tf_op jit(solution)/shard_map/mixed_backward/pallas_call | solution.py:379
  66.1 0.8 %copy.11 = bf16[1,128,2048]{2,1,0:T(8,128)(2,1)} copy(bf16[1,128,2048]{2,1,0:T(8,128)(2,1)S(1)} %bitcast.8) | data formatting | bytes 1048576
  66.9 1.0 %copy.12 = bf16[2,1,128,2048]{3,2,1,0:T(8,128)(2,1)} copy(bf16[2,1,128,2048]{3,2,1,0:T(8,128)(2,1)S(1)} %bitcast.7) | data formatting | bytes 2097152

commit v5 on v4

--- a/solution.py
+++ b/solution.py
@@ -13,7 +13,7 @@
 COUNT = WIDTH // CHUNK
 HEADS = WIDTH // HEAD_DIM
 LEAD = 8
-EARLY = 6
+EARLY = 4
 NEXT = 3
 BACK = 7
 HOME = 11
@@ -310,7 +310,6 @@
 
     for c in range(LEAD // 2, COUNT):
         kv_load(c).wait()
-    early(0, 2)
     for r in range(4):
         if r > 0:
             tags_to(4 - r).wait_recv()
@@ -330,11 +329,10 @@
 
     relay(0)
     project(0)
-    early(2, 4)
+    early(0, 3)
     relay(1)
     project(1)
-    early(4, EARLY)
-    relay(2)
+    early(3, EARLY)
 
     @pl.loop(0, (HEADS + HOME + 1) // 2)
     def _(j):
@@ -345,6 +343,7 @@
             pl.when(jnp.logical_and(u >= NEXT, u < HEADS + NEXT))(lambda: weigh(u - NEXT))
             pl.when(jnp.logical_and(u >= BACK, u < HEADS + BACK))(lambda: grads(u - BACK))
             if b == 0:
+                pl.when(j == 0)(lambda: relay(2))
                 pl.when(j + 2 < COUNT)(lambda: project(j + 2))
             else:
                 pl.when(j + 3 < COUNT)(lambda: relay(j + 3))

time: 68 us -> 68.8 us (1.012)
  Pallas kernels: 65.5 us -> 66.3 us
    pallas_call x1, Pallas kernels: 65.5 us -> 66.3 us  [shards(): pl.pallas_call(kernel, out_shape=(jax.ShapeDtypeStruct((ROWS, WIDTH), BF1...]
where the time goes in v5:
time: 68.8 us; the launch traced here: 68.7 us
  Pallas kernels  66.3 us (96%)
  local copies, waits for them, and re-layouts  1.77 us (3%)
    pallas_call x1, Pallas kernels, shards(): pl.pallas_call(kernel, out_shape=(jax.ShapeDtypeStruct((ROWS, WIDTH), BF1...  66.3 us
    unnamed x2, local copies, waits for them, and re-layouts  1.77 us

profile of v5, /device:TPU:24, one launch (start us, length us, event | category | flops | bytes accessed | tf_op | source)
XLA Modules:
  0.0 68.7 jit_solution(1673162113944107466)
XLA Ops:
  0.6 66.3 %mixed_backward.1 = (bf16[128,2048]{1,0:T(8,128)(2,1)S(1)}, bf16[2,128,2048]{2,1,0:T(8,128)(2,1)S(1)}) custom-call(bf16[128,2048]{1,0:T(8,128)(2,1)} %bitcast.10, bf16[2,128,2048]{2,1,0:T(8,128)(2,1)} %bitcast.9, bf16[128,2048]{1,0:T(8,128)(2,1)} %bitcast.11, s32[1,128]{1,0:T(1,128)} %tags_in.1, s32[1,2048]{1,0:T(1,128)} %seg_in.1, bf16[2,2048,128]{2,1,0:T(8,128)(2,1)} %w_in.1), custom_call_target="tpu_custom_call" | custom-call | tf_op jit(solution)/shard_map/mixed_backward/pallas_call | solution.py:378
  66.9 0.8 %copy.11 = bf16[1,128,2048]{2,1,0:T(8,128)(2,1)} copy(bf16[1,128,2048]{2,1,0:T(8,128)(2,1)S(1)} %bitcast.8) | data formatting | bytes 1048576
  67.7 1.0 %copy.12 = bf16[2,1,128,2048]{3,2,1,0:T(8,128)(2,1)} copy(bf16[2,1,128,2048]{3,2,1,0:T(8,128)(2,1)S(1)} %bitcast.7) | data formatting | bytes 2097152
